TPU v7x, 512 devices: a 4x2x32 block of a 4x8x32 slice. The times are simulated.
512 devices in a mesh: pairs: 2 (over y), gx: 32 (over z), gy: 4 (over x), gz: 2 (over core).
Axes of the slice: x: 4, y: 2, z: 32, core: 2. Of those that a mesh axis runs over, the one named last changes fastest.
The devices are a block of a 4x8x32 slice.
Arguments:
- fine_start: float32 [512, 256, 512], P(('pairs', 'gx'), 'gy', 'gz'), parts along dimension 0, may hold values from -1 to 1
- increments: float32 [2, 512, 256, 512], P(None, ('pairs', 'gx'), 'gy', 'gz'), parts along dimension 1, may hold values from -5 to 5
- coarse_start: float32 [256, 128, 256], P(('pairs', 'gx')), parts along dimension 0, may hold values from -1 to 1
Outputs:
- fine_final: float32 [512, 256, 512], P(('pairs', 'gx'), 'gy', 'gz'), parts along dimension 0
- coarse_final: float32 [256, 128, 256], P(('pairs', 'gx')), parts along dimension 0
There are 2 independent parts, one for each index of `pairs`. A program takes and returns all parts, laid end to end along the dimension named above; each array names one. Nothing has to cross between parts.
All inputs are finite; a program needn't handle non-finite values.
Results may differ from a plain program's by a relative error of at most 0.00002.
Values sent between devices are 32-bit elements; how exact they have to be, the bound alone decides.
A program may use at most 128 MiB of HBM per device.

v0:
```python
import jax
import jax.numpy as jnp
from jax import lax
from jax.sharding import PartitionSpec as P

STEPS = 2
SWEEPS = 2


noise_scale = 0.3
fine_step = 0.2
coarse_step = 0.4
fine_coupling = 1.0
coarse_coupling = 0.5


def with_halo(value, sides, width):
    for axis, dim in sides:
        count, length = (lax.axis_size(axis), value.shape[dim])
        up = [(i, (i + 1) % count) for i in range(count)]
        down = [(j, i) for i, j in up]
        last = lax.slice_in_dim(value, length - width, length, axis=dim)
        first = lax.slice_in_dim(value, 0, width, axis=dim)
        before = lax.ppermute(last, axis, up)
        after = lax.ppermute(first, axis, down)
        value = jnp.concatenate([before, value, after], axis=dim)
    return value


def joined_along(pieces, dim):
    lengths = list(pieces.shape[1:])
    lengths[dim] *= pieces.shape[0]
    return jnp.moveaxis(pieces, 0, dim).reshape(lengths)


def all_blocks(value, axes, turns):
    pieces = value
    for k in turns:
        pieces = lax.all_gather(pieces, axes[k])
    done = turns[::-1]
    back = [done.index(k) for k in range(len(axes))]
    pieces = pieces.transpose(*back, *range(len(axes), pieces.ndim))
    return pieces.reshape(-1, *value.shape)


def gathered_by_axis(value, axes, turns, dim):
    return joined_along(all_blocks(value, axes, turns), dim)


def neighbours(padded):
    beside = padded[2:, 1:-1, 1:-1] + padded[:-2, 1:-1, 1:-1]
    beside = beside + padded[1:-1, 2:, 1:-1] + padded[1:-1, :-2, 1:-1]
    beside = beside + padded[1:-1, 1:-1, 2:] + padded[1:-1, 1:-1, :-2]
    return beside


def trimmed_box(source, margin):
    return source[
        margin : source.shape[0] - margin,
        margin : source.shape[1] - margin,
        margin : source.shape[2] - margin,
    ]


def reaction(state, forcing, step_size):
    return state + step_size * (state - state * state * state) + noise_scale * forcing


def relaxed(source, coupling, extend):
    padded = extend(source, SWEEPS)
    fields = padded
    for sweep_index in range(SWEEPS):
        fields = (trimmed_box(padded, sweep_index + 1) + coupling * neighbours(fields)) / (
            1.0 + 6.0 * coupling
        )
    return fields


def fine_halo(source, width):
    return with_halo(source, (("gx", 0), ("gy", 1), ("gz", 2)), width)


def slab_halo(source, width):
    extended = with_halo(source, (("gx", 0),), width)
    return jnp.pad(extended, ((0, 0), (width, width), (width, width)), mode="wrap")


def assemble(stacked):
    count_y = lax.axis_size("gy")
    count_z = lax.axis_size("gz")
    depth_x, width_y, width_z = (stacked.shape[1], stacked.shape[2], stacked.shape[3])
    blocks = stacked.reshape(count_y, count_z, depth_x, width_y, width_z)
    return blocks.transpose(2, 0, 3, 1, 4).reshape(depth_x, count_y * width_y, count_z * width_z)


def body(fine_start, increments, coarse_start):
    state = fine_start
    for step_index in range(STEPS):
        state = relaxed(
            reaction(state, increments[step_index], fine_step), fine_coupling, fine_halo
        )
    summed = jnp.sum(increments, axis=0)
    half_x, half_y, half_z = (summed.shape[0] // 2, summed.shape[1] // 2, summed.shape[2] // 2)
    partial_value = 0.125 * summed.reshape(half_x, 2, half_y, 2, half_z, 2).sum(axis=(1, 3, 5))
    slab_noise = assemble(gathered_by_axis(partial_value[None], ("gy", "gz"), (0, 1), 0))
    coarse_final = relaxed(
        reaction(coarse_start, slab_noise, coarse_step), coarse_coupling, slab_halo
    )
    return (state, coarse_final)


def solution(mesh):
    return jax.shard_map(
        body,
        mesh=mesh,
        in_specs=(
            P(("pairs", "gx"), "gy", "gz"),
            P(None, ("pairs", "gx"), "gy", "gz"),
            P(("pairs", "gx"), None, None),
        ),
        out_specs=(P(("pairs", "gx"), "gy", "gz"), P(("pairs", "gx"), None, None)),
        check_vma=False,
    )
```

profile of v0, /device:TPU:33, one launch (start us, length us, event | category | flops | bytes accessed | tf_op | source)
XLA Modules:
  0.0 168.5 jit_solution(3886892721673093729)
XLA Ops:
  0.6 1.4 fusion.15
  2.1 0.7 fusion.34
  2.7 5.2 %collective-permute-start = (f32[2,64,256]{2,1,0:T(8,128)}, f32[2,64,256]{2,1,0:T(8,128)S(1)}, u32[]{:S(2)}, u32[]{:S(2)}) collective-permute-start(f32[2,64,256]{2,1,0:T(8,128)} %get-tuple-element.18), channel_id=1, source_target_pairs={{0,8},{8,16},{16,24},{24,32},{32,40},{40,48},{48,56},{56,64},{64,7... | collective-permute-start | bytes 393224 | tf_op jit(solution)/shard_map/ppermute | solution.py:24
  8.0 42.6 %collective-permute-start.1 = (f32[2,64,256]{2,1,0:T(8,128)S(1)}, f32[2,64,256]{2,1,0:T(8,128)S(1)}, u32[]{:S(2)}, u32[]{:S(2)}) collective-permute-start(f32[2,64,256]{2,1,0:T(8,128)S(1)} %get-tuple-element.19), channel_id=1, source_target_pairs={{8,0},{16,8},{24,16},{32,24},{40,32},{48,40},{56,48},{64,56},{72,6... | collective-permute-start | bytes 393224 | tf_op jit(solution)/shard_map/ppermute | solution.py:25
  50.7 34.8 %reshape.25 = f32[4,2,32,2,128,2]{5,4,3,2,1,0:T(8,128)} reshape(f32[8,64,256]{2,1,0:T(8,128)S(1)} %reduce_sum.18) | data formatting | bytes 1048576 | tf_op jit(solution)/shard_map/reshape | solution.py:104
  85.5 12.2 %reduce_sum.19 = f32[4,32,128]{2,1,0:T(8,128)S(1)} reduce(f32[4,2,32,2,128,2]{5,4,3,2,1,0:T(8,128)} %reshape.25, f32[]{:T(128)} %constant.6.clone.1), dimensions={1,3,5}, to_apply=%region_1.0 | reduce | flops 114688 | bytes 589828 | tf_op jit(solution)/shard_map/reduce_sum | solution.py:104
  97.8 11.0 %all-gather = f32[16,32,128]{2,1,0:T(8,128)S(1)} all-gather(f32[4,32,128]{2,1,0:T(8,128)S(1)} %broadcast_multiply_fusion), channel_id=2, replica_groups=mesh['pairs'=2,'gx'=32,'gy'=4,'gz'=2] {'gy'}, dimensions={0}, use_global_device_ids=true | all-gather | bytes 327680 | tf_op jit(solution)/shard_map/all_gather | solution.py:39
  108.7 4.7 %all-gather.1 = f32[8,1,4,32,128]{4,3,2,1,0:T(8,128)S(1)} all-gather(f32[4,1,4,32,128]{4,3,2,1,0:T(8,128)S(1)} %bitcast.17), channel_id=3, replica_groups=mesh['pairs'=2,'gx'=32,'gy'=4,'gz'=2] {'gz'}, dimensions={0}, use_global_device_ids=true | all-gather | bytes 786432 | tf_op jit(solution)/shard_map/all_gather | solution.py:39
  113.9 0.4 mul.110
  114.4 3.2 %collective-permute-start.2 = (f32[12,2,256]{2,1,0:T(2,128)S(1)}, f32[12,2,256]{2,1,0:T(2,128)S(1)}, u32[]{:S(2)}, u32[]{:S(2)}) collective-permute-start(f32[12,2,256]{2,1,0:T(2,128)S(1)} %get-tuple-element.12), channel_id=1, source_target_pairs={{0,2},{2,4},{4,6},{6,0},{1,3},{3,5},{5,7},{7,1},{8,10},{10,12},{12... | collective-permute-start | bytes 73736 | tf_op jit(solution)/shard_map/ppermute | solution.py:24
  117.6 3.3 %collective-permute-start.3 = (f32[12,2,256]{2,1,0:T(2,128)S(1)}, f32[12,2,256]{2,1,0:T(2,128)S(1)}, u32[]{:S(2)}, u32[]{:S(2)}) collective-permute-start(f32[12,2,256]{2,1,0:T(2,128)S(1)} %get-tuple-element.13), channel_id=1, source_target_pairs={{2,0},{4,2},{6,4},{0,6},{3,1},{5,3},{7,5},{1,7},{10,8},{12,10},{14... | collective-permute-start | bytes 73736 | tf_op jit(solution)/shard_map/ppermute | solution.py:25
  121.1 1.1 collective-permute-done.3
  122.5 3.7 %collective-permute-start.4 = (f32[12,68,2]{2,1,0:T(8,128)S(1)}, f32[12,68,2]{2,1,0:T(8,128)S(1)}, u32[]{:S(2)}, u32[]{:S(2)}) collective-permute-start(f32[12,68,2]{2,1,0:T(8,128)S(1)} %get-tuple-element.9), channel_id=1, source_target_pairs={{0,1},{1,0},{2,3},{3,2},{4,5},{5,4},{6,7},{7,6},{8,9},{9,8},{10,11... | collective-permute-start | bytes 19592 | tf_op jit(solution)/shard_map/ppermute | solution.py:24
  126.3 2.0 %collective-permute-start.5 = (f32[12,68,2]{2,1,0:T(8,128)S(1)}, f32[12,68,2]{2,1,0:T(8,128)S(1)}, u32[]{:S(2)}, u32[]{:S(2)}) collective-permute-start(f32[12,68,2]{2,1,0:T(8,128)S(1)} %get-tuple-element.8), channel_id=1, source_target_pairs={{1,0},{0,1},{3,2},{2,3},{5,4},{4,5},{7,6},{6,7},{9,8},{8,9},{11,10... | collective-permute-start | bytes 19592 | tf_op jit(solution)/shard_map/ppermute | solution.py:25
  128.3 2.0 %collective-permute-start.12 = (f32[2,128,256]{2,1,0:T(8,128)S(1)}, f32[2,128,256]{2,1,0:T(8,128)S(1)}, u32[]{:S(2)}, u32[]{:S(2)}) collective-permute-start(f32[2,128,256]{2,1,0:T(8,128)S(1)} %get-tuple-element.14), channel_id=1, source_target_pairs={{0,8},{8,16},{16,24},{24,32},{32,40},{40,48},{48,56},{56,64},{64,7... | collective-permute-start | bytes 786440 | tf_op jit(solution)/shard_map/ppermute | solution.py:24
  130.2 4.6 %collective-permute-start.13 = (f32[2,128,256]{2,1,0:T(8,128)S(1)}, f32[2,128,256]{2,1,0:T(8,128)S(1)}, u32[]{:S(2)}, u32[]{:S(2)}) collective-permute-start(f32[2,128,256]{2,1,0:T(8,128)S(1)} %get-tuple-element.15), channel_id=1, source_target_pairs={{8,0},{16,8},{24,16},{32,24},{40,32},{48,40},{56,48},{64,56},{72,6... | collective-permute-start | bytes 786440 | tf_op jit(solution)/shard_map/ppermute | solution.py:25
  134.9 0.6 pad_maximum_fusion.1
  135.5 1.9 %fusion.11 = f32[10,66,258]{2,1,0:T(8,128)S(1)} fusion(f32[12,68,2]{2,1,0:T(8,128)S(1)} %collective-permute-done.4, f32[12,2,256]{2,1,0:T(2,128)S(1)} %collective-permute-done.3, f32[12,2,256]{2,1,0:T(2,128)S(1)} %collective-permute-done.2, f32[2,64,256]{2,1,0:T(8,128)S(1)} %collective-permute-done.1, f32[8,64,256]{2,1,0:T(8,128)S(1)} %fusion.15, ...), kind=kLoop, calls=%fused_computation.42 | loop fusion | flops 2894760 | bytes 4935360 | tf_op jit(solution)/shard_map/div | solution.py:73
  137.4 0.8 fusion.18
  138.2 2.0 %collective-permute-start.6 = (f32[2,64,256]{2,1,0:T(8,128)S(1)}, f32[2,64,256]{2,1,0:T(8,128)S(1)}, u32[]{:S(2)}, u32[]{:S(2)}) collective-permute-start(f32[2,64,256]{2,1,0:T(8,128)S(1)} %get-tuple-element.16), channel_id=1, source_target_pairs={{0,8},{8,16},{16,24},{24,32},{32,40},{40,48},{48,56},{56,64},{64,7... | collective-permute-start | bytes 393224 | tf_op jit(solution)/shard_map/ppermute | solution.py:24
  140.2 4.6 %collective-permute-start.7 = (f32[2,64,256]{2,1,0:T(8,128)S(1)}, f32[2,64,256]{2,1,0:T(8,128)S(1)}, u32[]{:S(2)}, u32[]{:S(2)}) collective-permute-start(f32[2,64,256]{2,1,0:T(8,128)S(1)} %get-tuple-element.17), channel_id=1, source_target_pairs={{8,0},{16,8},{24,16},{32,24},{40,32},{48,40},{56,48},{64,56},{72,6... | collective-permute-start | bytes 393224 | tf_op jit(solution)/shard_map/ppermute | solution.py:25
  145.2 0.7 pad_maximum_fusion
  146.0 0.8 collective-permute-done.7
  146.8 2.3 %collective-permute-start.8 = (f32[12,2,256]{2,1,0:T(2,128)S(1)}, f32[12,2,256]{2,1,0:T(2,128)S(1)}, u32[]{:S(2)}, u32[]{:S(2)}) collective-permute-start(f32[12,2,256]{2,1,0:T(2,128)S(1)} %get-tuple-element.10), channel_id=1, source_target_pairs={{0,2},{2,4},{4,6},{6,0},{1,3},{3,5},{5,7},{7,1},{8,10},{10,12},{12... | collective-permute-start | bytes 73736 | tf_op jit(solution)/shard_map/ppermute | solution.py:24
  149.0 4.5 %collective-permute-start.9 = (f32[12,2,256]{2,1,0:T(2,128)S(1)}, f32[12,2,256]{2,1,0:T(2,128)S(1)}, u32[]{:S(2)}, u32[]{:S(2)}) collective-permute-start(f32[12,2,256]{2,1,0:T(2,128)S(1)} %get-tuple-element.11), channel_id=1, source_target_pairs={{2,0},{4,2},{6,4},{0,6},{3,1},{5,3},{7,5},{1,7},{10,8},{12,10},{14... | collective-permute-start | bytes 73736 | tf_op jit(solution)/shard_map/ppermute | solution.py:25
  153.5 2.1 %fusion.3 = f32[6,130,258]{2,1,0:T(8,128)S(1)} fusion(f32[8,132,2]{2,1,0:T(8,128)S(1)} %get-tuple-element.3, f32[8,2,256]{2,1,0:T(2,128)S(1)} %get-tuple-element.5, f32[8,2,256]{2,1,0:T(2,128)S(1)} %get-tuple-element.4, f32[2,128,256]{2,1,0:T(8,128)S(1)} %collective-permute-done.13, f32[4,128,256]{2,1,0:T(8,128)S(1)} %fusion.21, ...), kind=kLoop, calls=%fused_computation.7 | loop fusion | flops 3622320 | bytes 5928000 | tf_op jit(solution)/shard_map/div | solution.py:73
  156.0 4.7 %collective-permute-start.10 = (f32[12,68,2]{2,1,0:T(8,128)S(1)}, f32[12,68,2]{2,1,0:T(8,128)S(1)}, u32[]{:S(2)}, u32[]{:S(2)}) collective-permute-start(f32[12,68,2]{2,1,0:T(8,128)S(1)} %get-tuple-element.7), channel_id=1, source_target_pairs={{0,1},{1,0},{2,3},{3,2},{4,5},{5,4},{6,7},{7,6},{8,9},{9,8},{10,11... | collective-permute-start | bytes 19592 | tf_op jit(solution)/shard_map/ppermute | solution.py:24
  160.6 2.0 %collective-permute-start.11 = (f32[12,68,2]{2,1,0:T(8,128)S(1)}, f32[12,68,2]{2,1,0:T(8,128)S(1)}, u32[]{:S(2)}, u32[]{:S(2)}) collective-permute-start(f32[12,68,2]{2,1,0:T(8,128)S(1)} %get-tuple-element.6), channel_id=1, source_target_pairs={{1,0},{0,1},{3,2},{2,3},{5,4},{4,5},{7,6},{6,7},{9,8},{8,9},{11,10... | collective-permute-start | bytes 19592 | tf_op jit(solution)/shard_map/ppermute | solution.py:25
  162.6 1.5 fusion.24
  164.4 0.6 pad_maximum_fusion.2
  165.0 1.9 %fusion.7 = f32[10,66,258]{2,1,0:T(8,128)S(1)} fusion(f32[12,68,2]{2,1,0:T(8,128)S(1)} %collective-permute-done.10, f32[12,2,256]{2,1,0:T(2,128)S(1)} %collective-permute-done.9, f32[12,2,256]{2,1,0:T(2,128)S(1)} %collective-permute-done.8, f32[2,64,256]{2,1,0:T(8,128)S(1)} %collective-permute-done.7, f32[8,64,256]{2,1,0:T(8,128)S(1)} %fusion.18, ...), kind=kLoop, calls=%fused_computation.25 | loop fusion | flops 2894760 | bytes 4935360 | tf_op jit(solution)/shard_map/div | solution.py:73
  166.9 1.6 fusion.26
  (32 shorter events, 2.0 us)
Async XLA Ops:
  0.6 49.9 %copy-start = (f32[2,8,64,256]{3,2,1,0:T(8,128)S(1)}, f32[2,8,64,256]{3,2,1,0:T(8,128)}, u32[]{:S(2)}) copy-start(f32[2,8,64,256]{3,2,1,0:T(8,128)} %param.4) | copy-start | bytes 3145732
  2.7 111.6 %collective-permute-start = (f32[2,64,256]{2,1,0:T(8,128)}, f32[2,64,256]{2,1,0:T(8,128)S(1)}, u32[]{:S(2)}, u32[]{:S(2)}) collective-permute-start(f32[2,64,256]{2,1,0:T(8,128)} %get-tuple-element.18), channel_id=1, source_target_pairs={{0,8},{8,16},{16,24},{24,32},{32,40},{40,48},{48,56},{56,64},{64,7... | collective-permute-start | bytes 393224 | tf_op jit(solution)/shard_map/ppermute | solution.py:24
  8.0 106.4 %collective-permute-start.1 = (f32[2,64,256]{2,1,0:T(8,128)S(1)}, f32[2,64,256]{2,1,0:T(8,128)S(1)}, u32[]{:S(2)}, u32[]{:S(2)}) collective-permute-start(f32[2,64,256]{2,1,0:T(8,128)S(1)} %get-tuple-element.19), channel_id=1, source_target_pairs={{8,0},{16,8},{24,16},{32,24},{40,32},{48,40},{56,48},{64,56},{72,6... | collective-permute-start | bytes 393224 | tf_op jit(solution)/shard_map/ppermute | solution.py:25
  113.5 7.5 %copy-start.1 = (f32[4,128,256]{2,1,0:T(8,128)S(1)}, f32[4,128,256]{2,1,0:T(8,128)}, u32[]{:S(2)}) copy-start(f32[4,128,256]{2,1,0:T(8,128)} %param.5) | copy-start | bytes 1572868
  114.4 6.7 %collective-permute-start.2 = (f32[12,2,256]{2,1,0:T(2,128)S(1)}, f32[12,2,256]{2,1,0:T(2,128)S(1)}, u32[]{:S(2)}, u32[]{:S(2)}) collective-permute-start(f32[12,2,256]{2,1,0:T(2,128)S(1)} %get-tuple-element.12), channel_id=1, source_target_pairs={{0,2},{2,4},{4,6},{6,0},{1,3},{3,5},{5,7},{7,1},{8,10},{10,12},{12... | collective-permute-start | bytes 73736 | tf_op jit(solution)/shard_map/ppermute | solution.py:24
  117.6 4.6 %collective-permute-start.3 = (f32[12,2,256]{2,1,0:T(2,128)S(1)}, f32[12,2,256]{2,1,0:T(2,128)S(1)}, u32[]{:S(2)}, u32[]{:S(2)}) collective-permute-start(f32[12,2,256]{2,1,0:T(2,128)S(1)} %get-tuple-element.13), channel_id=1, source_target_pairs={{2,0},{4,2},{6,4},{0,6},{3,1},{5,3},{7,5},{1,7},{10,8},{12,10},{14... | collective-permute-start | bytes 73736 | tf_op jit(solution)/shard_map/ppermute | solution.py:25
  122.5 12.3 %collective-permute-start.4 = (f32[12,68,2]{2,1,0:T(8,128)S(1)}, f32[12,68,2]{2,1,0:T(8,128)S(1)}, u32[]{:S(2)}, u32[]{:S(2)}) collective-permute-start(f32[12,68,2]{2,1,0:T(8,128)S(1)} %get-tuple-element.9), channel_id=1, source_target_pairs={{0,1},{1,0},{2,3},{3,2},{4,5},{5,4},{6,7},{7,6},{8,9},{9,8},{10,11... | collective-permute-start | bytes 19592 | tf_op jit(solution)/shard_map/ppermute | solution.py:24
  126.3 8.6 %collective-permute-start.5 = (f32[12,68,2]{2,1,0:T(8,128)S(1)}, f32[12,68,2]{2,1,0:T(8,128)S(1)}, u32[]{:S(2)}, u32[]{:S(2)}) collective-permute-start(f32[12,68,2]{2,1,0:T(8,128)S(1)} %get-tuple-element.8), channel_id=1, source_target_pairs={{1,0},{0,1},{3,2},{2,3},{5,4},{4,5},{7,6},{6,7},{9,8},{8,9},{11,10... | collective-permute-start | bytes 19592 | tf_op jit(solution)/shard_map/ppermute | solution.py:25
  128.3 16.6 %collective-permute-start.12 = (f32[2,128,256]{2,1,0:T(8,128)S(1)}, f32[2,128,256]{2,1,0:T(8,128)S(1)}, u32[]{:S(2)}, u32[]{:S(2)}) collective-permute-start(f32[2,128,256]{2,1,0:T(8,128)S(1)} %get-tuple-element.14), channel_id=1, source_target_pairs={{0,8},{8,16},{16,24},{24,32},{32,40},{40,48},{48,56},{56,64},{64,7... | collective-permute-start | bytes 786440 | tf_op jit(solution)/shard_map/ppermute | solution.py:24
  130.2 14.6 %collective-permute-start.13 = (f32[2,128,256]{2,1,0:T(8,128)S(1)}, f32[2,128,256]{2,1,0:T(8,128)S(1)}, u32[]{:S(2)}, u32[]{:S(2)}) collective-permute-start(f32[2,128,256]{2,1,0:T(8,128)S(1)} %get-tuple-element.15), channel_id=1, source_target_pairs={{8,0},{16,8},{24,16},{32,24},{40,32},{48,40},{56,48},{64,56},{72,6... | collective-permute-start | bytes 786440 | tf_op jit(solution)/shard_map/ppermute | solution.py:25
  138.2 7.7 %collective-permute-start.6 = (f32[2,64,256]{2,1,0:T(8,128)S(1)}, f32[2,64,256]{2,1,0:T(8,128)S(1)}, u32[]{:S(2)}, u32[]{:S(2)}) collective-permute-start(f32[2,64,256]{2,1,0:T(8,128)S(1)} %get-tuple-element.16), channel_id=1, source_target_pairs={{0,8},{8,16},{16,24},{24,32},{32,40},{40,48},{48,56},{56,64},{64,7... | collective-permute-start | bytes 393224 | tf_op jit(solution)/shard_map/ppermute | solution.py:24
  140.2 6.5 %collective-permute-start.7 = (f32[2,64,256]{2,1,0:T(8,128)S(1)}, f32[2,64,256]{2,1,0:T(8,128)S(1)}, u32[]{:S(2)}, u32[]{:S(2)}) collective-permute-start(f32[2,64,256]{2,1,0:T(8,128)S(1)} %get-tuple-element.17), channel_id=1, source_target_pairs={{8,0},{16,8},{24,16},{32,24},{40,32},{48,40},{56,48},{64,56},{72,6... | collective-permute-start | bytes 393224 | tf_op jit(solution)/shard_map/ppermute | solution.py:25
  146.8 8.9 %collective-permute-start.8 = (f32[12,2,256]{2,1,0:T(2,128)S(1)}, f32[12,2,256]{2,1,0:T(2,128)S(1)}, u32[]{:S(2)}, u32[]{:S(2)}) collective-permute-start(f32[12,2,256]{2,1,0:T(2,128)S(1)} %get-tuple-element.10), channel_id=1, source_target_pairs={{0,2},{2,4},{4,6},{6,0},{1,3},{3,5},{5,7},{7,1},{8,10},{10,12},{12... | collective-permute-start | bytes 73736 | tf_op jit(solution)/shard_map/ppermute | solution.py:24
  149.0 6.6 %collective-permute-start.9 = (f32[12,2,256]{2,1,0:T(2,128)S(1)}, f32[12,2,256]{2,1,0:T(2,128)S(1)}, u32[]{:S(2)}, u32[]{:S(2)}) collective-permute-start(f32[12,2,256]{2,1,0:T(2,128)S(1)} %get-tuple-element.11), channel_id=1, source_target_pairs={{2,0},{4,2},{6,4},{0,6},{3,1},{5,3},{7,5},{1,7},{10,8},{12,10},{14... | collective-permute-start | bytes 73736 | tf_op jit(solution)/shard_map/ppermute | solution.py:25
  156.0 8.2 %collective-permute-start.10 = (f32[12,68,2]{2,1,0:T(8,128)S(1)}, f32[12,68,2]{2,1,0:T(8,128)S(1)}, u32[]{:S(2)}, u32[]{:S(2)}) collective-permute-start(f32[12,68,2]{2,1,0:T(8,128)S(1)} %get-tuple-element.7), channel_id=1, source_target_pairs={{0,1},{1,0},{2,3},{3,2},{4,5},{5,4},{6,7},{7,6},{8,9},{9,8},{10,11... | collective-permute-start | bytes 19592 | tf_op jit(solution)/shard_map/ppermute | solution.py:24
  160.6 3.7 %collective-permute-start.11 = (f32[12,68,2]{2,1,0:T(8,128)S(1)}, f32[12,68,2]{2,1,0:T(8,128)S(1)}, u32[]{:S(2)}, u32[]{:S(2)}) collective-permute-start(f32[12,68,2]{2,1,0:T(8,128)S(1)} %get-tuple-element.6), channel_id=1, source_target_pairs={{1,0},{0,1},{3,2},{2,3},{5,4},{4,5},{7,6},{6,7},{9,8},{8,9},{11,10... | collective-permute-start | bytes 19592 | tf_op jit(solution)/shard_map/ppermute | solution.py:25
where the time goes:
time: 169 us
  starting transfers between devices  86.5 us (51%)
  local copies, waits for them, and re-layouts  37 us (22%)
  other arithmetic  26.2 us (16%)
  blocking collectives  15.6 us (9%)
  waiting for transfers between devices  2.14 us (1%)
    ppermute x7, starting transfers between devices, with_halo(): after = lax.ppermute(first, axis, down)  63.5 us
    reshape x1, local copies, waits for them, and re-layouts, body(): summed.reshape(half_x, 2, half_y, 2, half_z, 2).sum(axis=(1, 3, 5))  34.8 us
    ppermute x7, starting transfers between devices, with_halo(): before = lax.ppermute(last, axis, up)  23.1 us
    all_gather x2, blocking collectives, all_blocks(): pieces = lax.all_gather(pieces, axes[k])  15.6 us
    reduce_sum x1, other arithmetic, body(): summed.reshape(half_x, 2, half_y, 2, half_z, 2).sum(axis=(1, 3, 5))  12.2 us
    div x5, other arithmetic, relaxed(): (trimmed_box(padded, sweep_index + 1) + coupling * neighbours(fields)) /...  9.08 us
  transfers between devices with their start and end apart: 14, of which 3 were waited for; matrix products, arithmetic and copies ran while one was open for 33% of the time, Pallas kernels for 0%

commit v1 on v0

v1 whole, which is shorter than its diff:
```python
import functools

import jax
import jax.numpy as jnp
from jax import lax
from jax.experimental import pallas as pl
from jax.experimental.pallas import tpu as pltpu
from jax.sharding import PartitionSpec as P

MESH = pl.DeviceIdType.MESH
NOISE = 0.3
FINE_STEP = 0.2
COARSE_STEP = 0.4
COARSE_COUPLING = 0.5
FINE_SCALE = 1.0 / 7.0
COARSE_SCALE = 1.0 / 4.0


def reaction(state, forcing, step):
    return state + step * (state - state * state * state) + NOISE * forcing


def ring_sum(center):
    rows, lanes = center.shape
    beside = pltpu.roll(center, rows - 1, 0) + pltpu.roll(center, 1, 0)
    return beside + (pltpu.roll(center, lanes - 1, 1) + pltpu.roll(center, 1, 1))


def kernel(sizes, u_hbm, e_hbm, cs_hbm, fo, co, u, e, cs, v1, v2, w, zs1, zs2, pks, pkr,
           sums, c, cw, cblk, load_sem, send_sem, recv_sem):
    n_gx, n_gy, n_gz = sizes
    X, Y, Z = u.shape
    CX, CY, CZ = cs.shape
    me_x, me_y, me_z = lax.axis_index("gx"), lax.axis_index("gy"), lax.axis_index("gz")
    R, L = lax.rem(me_x + 1, n_gx), lax.rem(me_x + n_gx - 1, n_gx)
    U, D = lax.rem(me_y + 1, n_gy), lax.rem(me_y + n_gy - 1, n_gy)
    O = lax.rem(me_y + 2, n_gy)
    Q = lax.rem(me_z + 1, n_gz)

    def dev(x=None, y=None, z=None):
        return {"gx": me_x if x is None else x, "gy": me_y if y is None else y,
                "gz": me_z if z is None else z}

    loads = []

    def load(src, dst):
        k = len(loads)
        copy = pltpu.make_async_copy(src, dst, load_sem.at[k])
        copy.start()
        loads.append(copy)
        return copy

    lu0, le0 = load(u_hbm.at[0:2], u.at[0:2]), load(e_hbm.at[0, 0:2], e.at[0, 0:2])
    lu3, le3 = load(u_hbm.at[X - 2 : X], u.at[X - 2 : X]), load(e_hbm.at[0, X - 2 : X], e.at[0, X - 2 : X])
    le1 = load(e_hbm.at[1], e.at[1])
    lem = load(e_hbm.at[0, 2 : X - 2], e.at[0, 2 : X - 2])
    own_y = pl.ds(pl.multiple_of(me_y * CY, 8), CY)
    own_z = pl.ds(pl.multiple_of(me_z * CZ, 128), CZ)
    lcs = load(cs_hbm.at[:, own_y, own_z], cs)
    lum = load(u_hbm.at[2 : X - 2], u.at[2 : X - 2])

    barrier = pltpu.get_barrier_semaphore()
    partners = [dev(x=R), dev(x=L), dev(x=R, z=Q), dev(x=L, z=Q),
                dev(x=R, y=U), dev(x=R, y=D), dev(x=L, y=U), dev(x=L, y=D),
                dev(y=U), dev(y=D), dev(y=U, z=Q), dev(y=D, z=Q), dev(z=Q), dev(y=O)]
    for partner in partners:
        pl.semaphore_signal(barrier, inc=1, device_id=partner, device_id_type=MESH)

    sends = []

    def send(src, dst, to):
        k = len(sends)
        copy = pltpu.make_async_remote_copy(
            src_ref=src, dst_ref=dst, send_sem=send_sem.at[k], recv_sem=recv_sem.at[k],
            device_id=to, device_id_type=MESH)
        copy.start()
        sends.append(copy)
        return copy

    lane = lax.broadcasted_iota(jnp.int32, (Y, 128), 1)

    def first_advance(x):
        v1[2 + x, 0:Y, 0:Z] = reaction(u[x], e[0, x], FINE_STEP)

    def z_select(v, zs, x):
        zs[x] = jnp.where(lane < 64, v[2 + x, 0:Y, 0:128], v[2 + x, 0:Y, Z - 128 : Z])

    def pack(v, slot):
        columns = [
            jnp.where(lane == 0, v[2 + x, 0:Y, 0:128], pltpu.roll(v[2 + x, 0:Y, Z - 128 : Z], 8, 1))
            for x in (0, X - 1)
        ]
        pks[slot] = jnp.transpose(jnp.concatenate(columns, axis=0))[0:8, :]

    def unpack(v, slot):
        from_left = jnp.transpose(jnp.concatenate([pkr[slot, 0]] * 16, axis=0))
        from_right = jnp.transpose(jnp.concatenate([pkr[slot, 1]] * 16, axis=0))
        v[1, 0:Y, Z : Z + 128] = from_left[Y : 2 * Y, :]
        v[X + 2, 0:Y, Z : Z + 128] = from_right[0:Y, :]

    def send_near(v):
        return [send(v.at[X + 1, 0:Y, 0:Z], v.at[1, 0:Y, 0:Z], dev(x=R)),
                send(v.at[2, 0:Y, 0:Z], v.at[X + 2, 0:Y, 0:Z], dev(x=L))]

    def send_far(v):
        return [send(v.at[X, 0:Y, 0:Z], v.at[0, 0:Y, 0:Z], dev(x=R)),
                send(v.at[3, 0:Y, 0:Z], v.at[X + 3, 0:Y, 0:Z], dev(x=L))]

    def send_diagonals(v, slot):
        out = []
        for mine, theirs, x in ((X + 1, 1, R), (2, X + 2, L)):
            out.append(send(v.at[mine, Y - 1 : Y, 0:Z], v.at[theirs, Y + 7 : Y + 8, 0:Z], dev(x=x, y=U)))
            out.append(send(v.at[mine, 0:1, 0:Z], v.at[theirs, Y : Y + 1, 0:Z], dev(x=x, y=D)))
        out.append(send(pks.at[slot], pkr.at[slot, 0], dev(x=R, z=Q)))
        out.append(send(pks.at[slot], pkr.at[slot, 1], dev(x=L, z=Q)))
        return out

    def send_sides(v, zs, first, last):
        xs, ext = slice(first, last), slice(first + 2, last + 2)
        return [
            send(zs.at[xs], v.at[ext, 0:Y, Z : Z + 128], dev(z=Q)),
            send(v.at[ext, Y - 2 : Y, 0:Z], v.at[ext, Y + 6 : Y + 8, 0:Z], dev(y=U)),
            send(v.at[ext, 0:2, 0:Z], v.at[ext, Y : Y + 2, 0:Z], dev(y=D)),
            send(zs.at[xs, Y - 2 : Y], v.at[ext, Y + 6 : Y + 8, Z : Z + 128], dev(y=U, z=Q)),
            send(zs.at[xs, 0:2], v.at[ext, Y : Y + 2, Z : Z + 128], dev(y=D, z=Q)),
        ]

    def wait(copies):
        for copy in copies:
            copy.wait_recv()

    def sweep_one(v, k):
        center = v[k]
        w[k - 1] = (center + (v[k + 1] + v[k - 1] + ring_sum(center))) * FINE_SCALE

    def sweep_one_own(v, k):
        center = v[k]
        beside = v[k + 1, 0:Y, 0:Z] + v[k - 1, 0:Y, 0:Z] + ring_sum(center)[0:Y, 0:Z]
        w[k - 1, 0:Y, 0:Z] = (center[0:Y, 0:Z] + beside) * FINE_SCALE

    def sweep_two(v, k):
        beside = w[k, 0:Y, 0:Z] + w[k - 2, 0:Y, 0:Z] + ring_sum(w[k - 1])[0:Y, 0:Z]
        return (v[k, 0:Y, 0:Z] + beside) * FINE_SCALE

    def second_advance(k):
        v2[k, 0:Y, 0:Z] = reaction(sweep_two(v1, k), e[1, k - 2], FINE_STEP)

    def planes(first, last, body):
        def step(k, carry):
            body(k)
            return carry
        lax.fori_loop(first, last, step, 0)

    lu0.wait()
    le0.wait()
    first_advance(0)
    lu3.wait()
    le3.wait()
    first_advance(X - 1)
    pl.semaphore_wait(barrier, len(partners))
    near1 = send_near(v1)

    le1.wait()
    lem.wait()
    for x in range(CX):
        total = (e[0, 2 * x] + e[0, 2 * x + 1]) + (e[1, 2 * x] + e[1, 2 * x + 1])
        for t in range(Z // 128):
            sums[t, x * Y : (x + 1) * Y, :] = total[:, t * 128 : (t + 1) * 128]
    pairs = [sums[t, pl.ds(0, CX * CY, stride=2), :] + sums[t, pl.ds(1, CX * CY, stride=2), :]
             for t in range(Z // 128)]
    halve = (lax.broadcasted_iota(jnp.int32, (Z, CZ), 0) // 2
             == lax.broadcasted_iota(jnp.int32, (Z, CZ), 1)).astype(jnp.float32)
    noise = 0.125 * jnp.dot(jnp.concatenate(pairs, axis=1), halve,
                            precision=lax.Precision.HIGHEST, preferred_element_type=jnp.float32)
    lcs.wait()
    c[2 : CX + 2, 0:CY, 0:CZ] = reaction(cs[...], noise.reshape(CX, CY, CZ), COARSE_STEP)
    coarse_x = [
        send(c.at[CX : CX + 2, 0:CY, 0:CZ], c.at[0:2, 0:CY, 0:CZ], dev(x=R)),
        send(c.at[2:4, 0:CY, 0:CZ], c.at[CX + 2 : CX + 4, 0:CY, 0:CZ], dev(x=L)),
        send(c.at[CX + 1, 0:CY, 0:CZ], c.at[1, 0:CY, CZ : 2 * CZ], dev(x=R, z=Q)),
        send(c.at[2, 0:CY, 0:CZ], c.at[CX + 2, 0:CY, CZ : 2 * CZ], dev(x=L, z=Q)),
    ]
    for mine, theirs, x in ((CX + 1, 1, R), (2, CX + 2, L)):
        coarse_x.append(send(c.at[mine, CY - 1 : CY, 0:CZ], c.at[theirs, CY + 7 : CY + 8, 0:CZ], dev(x=x, y=U)))
        coarse_x.append(send(c.at[mine, 0:1, 0:CZ], c.at[theirs, CY : CY + 1, 0:CZ], dev(x=x, y=D)))
    inner = slice(2, CX + 2)
    coarse_yz = [
        send(c.at[inner, 0:CY, 0:CZ], c.at[inner, 0:CY, CZ : 2 * CZ], dev(z=Q)),
        send(c.at[inner, CY - 2 : CY, 0:CZ], c.at[inner, CY + 6 : CY + 8, 0:CZ], dev(y=U)),
        send(c.at[inner, 0:2, 0:CZ], c.at[inner, CY : CY + 2, 0:CZ], dev(y=D)),
        send(c.at[inner, CY - 1 : CY, 0:CZ], c.at[inner, CY + 7 : CY + 8, CZ : 2 * CZ], dev(y=U, z=Q)),
        send(c.at[inner, 0:1, 0:CZ], c.at[inner, CY : CY + 1, CZ : 2 * CZ], dev(y=D, z=Q)),
    ]

    first_advance(1)
    first_advance(X - 2)
    far1 = send_far(v1)
    pack(v1, 0)
    diag1 = send_diagonals(v1, 0)
    lum.wait()
    planes(2, X - 2, first_advance)
    planes(0, X, lambda x: z_select(v1, zs1, x))
    sides1 = send_sides(v1, zs1, 0, X)

    wait(sides1)
    planes(3, X + 1, lambda k: sweep_one(v1, k))
    planes(4, X, second_advance)

    wait(near1)
    for k in (2, X + 1):
        sweep_one_own(v1, k)
    for k in (3, X):
        second_advance(k)
    far2 = send_far(v2)
    planes(1, X - 1, lambda x: z_select(v2, zs2, x))
    inside2 = send_sides(v2, zs2, 1, X - 1)

    wait(coarse_yz)
    wait(coarse_x)
    for k in range(1, CX + 3):
        center = c[k]
        beside = c[k + 1] + c[k - 1] + ring_sum(center)
        cw[k - 1] = (center + COARSE_COUPLING * beside) * COARSE_SCALE
    for k in range(2, CX + 2):
        beside = cw[k, 0:CY, 0:CZ] + cw[k - 2, 0:CY, 0:CZ] + ring_sum(cw[k - 1])[0:CY, 0:CZ]
        cblk[k - 2] = (c[k, 0:CY, 0:CZ] + COARSE_COUPLING * beside) * COARSE_SCALE
    mine = co.at[:, own_y, own_z]
    gather = [send(cblk, mine, dev(y=O)), send(cblk, mine, dev(y=U)), send(cblk, mine, dev(y=D))]
    direct = send(cblk, mine, dev(z=Q))
    co[:, own_y, own_z] = cblk[...]

    wait(far1)
    wait(diag1)
    unpack(v1, 0)
    for k in (1, X + 2):
        sweep_one_own(v1, k)
    for k in (2, X + 1):
        sweep_one(v1, k)
    for k in (2, X + 1):
        second_advance(k)
    near2 = send_near(v2)
    pack(v2, 1)
    diag2 = send_diagonals(v2, 1)
    z_select(v2, zs2, 0)
    z_select(v2, zs2, X - 1)
    outside2 = send_sides(v2, zs2, 0, 1) + send_sides(v2, zs2, X - 1, X)

    wait(inside2)
    planes(4, X, lambda k: sweep_one(v2, k))

    def finish(k):
        fo[k - 2] = sweep_two(v2, k)

    planes(5, X - 1, finish)

    passed = []
    for copy, owner in ((gather[1], D), (gather[2], U), (gather[0], O)):
        copy.wait_recv()
        block = co.at[:, pl.ds(pl.multiple_of(owner * CY, 8), CY), own_z]
        passed.append(send(block, block, dev(z=Q)))

    wait(outside2)
    for k in (3, X):
        sweep_one(v2, k)
    for k in (4, X - 1):
        finish(k)
    wait(far2)
    wait(near2)
    wait(diag2)
    unpack(v2, 1)
    for k in (1, X + 2):
        sweep_one_own(v2, k)
    for k in (2, X + 1):
        sweep_one(v2, k)
    for k in (2, 3, X, X + 1):
        finish(k)

    direct.wait_recv()
    wait(passed)
    for copy in sends:
        copy.wait_send()


N_MESSAGES = 64


def body(sizes, fine_start, increments, coarse_start):
    X, Y, Z = fine_start.shape
    CX, CY, CZ = X // 2, Y // 2, Z // 2
    f32 = jnp.float32
    any_space = pl.BlockSpec(memory_space=pl.ANY)
    in_vmem = pl.BlockSpec(memory_space=pltpu.VMEM)
    fine, coarse = pl.pallas_call(
        functools.partial(kernel, sizes),
        out_shape=(pltpu.VMEM((X, Y, Z), f32), pltpu.VMEM(coarse_start.shape, f32)),
        in_specs=[any_space] * 3,
        out_specs=(in_vmem, in_vmem),
        scratch_shapes=[
            pltpu.VMEM((X, Y, Z), f32),
            pltpu.VMEM((2, X, Y, Z), f32),
            pltpu.VMEM((CX, CY, CZ), f32),
            pltpu.VMEM((X + 4, Y + 8, Z + 128), f32),
            pltpu.VMEM((X + 4, Y + 8, Z + 128), f32),
            pltpu.VMEM((X + 2, Y + 8, Z + 128), f32),
            pltpu.VMEM((X, Y, 128), f32),
            pltpu.VMEM((X, Y, 128), f32),
            pltpu.VMEM((2, 8, 128), f32),
            pltpu.VMEM((2, 2, 8, 128), f32),
            pltpu.VMEM((Z // 128, CX * Y, 128), f32),
            pltpu.VMEM((CX + 4, CY + 8, 2 * CZ), f32),
            pltpu.VMEM((CX + 2, CY + 8, 2 * CZ), f32),
            pltpu.VMEM((CX, CY, CZ), f32),
            pltpu.SemaphoreType.DMA((8,)),
            pltpu.SemaphoreType.DMA((N_MESSAGES,)),
            pltpu.SemaphoreType.DMA((N_MESSAGES,)),
        ],
        compiler_params=pltpu.CompilerParams(collective_id=0, has_side_effects=True),
    )(fine_start, increments, coarse_start)
    return fine, coarse


def solution(mesh):
    sizes = tuple(mesh.shape[name] for name in ("gx", "gy", "gz"))
    return jax.shard_map(
        functools.partial(body, sizes),
        mesh=mesh,
        in_specs=(
            P(("pairs", "gx"), "gy", "gz"),
            P(None, ("pairs", "gx"), "gy", "gz"),
            P(("pairs", "gx"), None, None),
        ),
        out_specs=(P(("pairs", "gx"), "gy", "gz"), P(("pairs", "gx"), None, None)),
        check_vma=False,
    )
```

time: 169 us -> 64.5 us (0.38)
  starting transfers between devices: 86.5 us -> 0 us
  Pallas kernels: 0 us -> 62.1 us
  local copies, waits for them, and re-layouts: 37 us -> 1.59 us
  other arithmetic: 26.2 us -> 0 us
  blocking collectives: 15.6 us -> 0 us
  waiting for transfers between devices: 2.14 us -> 0 us
    ppermute x14 -> x0, starting transfers between devices: 86.5 us -> none  [the longest x7 63.5 us: with_halo(): after = lax.ppermute(first, axis, down)]
    pallas_call x0 -> x1, Pallas kernels: none -> 62.1 us  [body(): pl.pallas_call(functools.partial(kernel, sizes), out_shape=(pltpu.VMEM((X...]
    reshape x1 -> x0, local copies, waits for them, and re-layouts: 34.8 us -> none  [body(): summed.reshape(half_x, 2, half_y, 2, half_z, 2).sum(axis=(1, 3, 5))]
    all_gather x2 -> x0, blocking collectives: 15.6 us -> none  [all_blocks(): pieces = lax.all_gather(pieces, axes[k])]
    reduce_sum x2 -> x0, other arithmetic: 12.3 us -> none  [the longest x1 12.2 us: body(): summed.reshape(half_x, 2, half_y, 2, half_z, 2).sum(axis=(1, 3, 5))]
    div x5 -> x0, other arithmetic: 9.08 us -> none  [relaxed(): (trimmed_box(padded, sweep_index + 1) + coupling * neighbours(fields)) /...]
    concatenate x6 -> x0, other arithmetic: 2.38 us -> none  [the longest x4 1.49 us: with_halo(): value = jnp.concatenate([before, value, after], axis=dim)]
    add x3 -> x0, other arithmetic: 2.3 us -> none  [reaction(): state + step_size * (state - state * state * state) + noise_scale * forcing]
  transfers between devices with their start and end apart: 14 -> 0, of which waited for: 3 -> 0; matrix products, arithmetic and copies ran while one was open for 33% -> 0% of each run, Pallas kernels for 0% -> 0%
where the time goes in v1:
time: 64.5 us; the launch traced here: 64.4 us
  Pallas kernels  62.1 us (96%)
  local copies, waits for them, and re-layouts  1.59 us (2%)
    pallas_call x1, Pallas kernels, body(): pl.pallas_call(functools.partial(kernel, sizes), out_shape=(pltpu.VMEM((X...  62.1 us
    unnamed x2, local copies, waits for them, and re-layouts  1.59 us

profile of v1, /device:TPU:33, one launch (start us, length us, event | category | flops | bytes accessed | tf_op | source)
XLA Modules:
  0.0 64.4 jit_solution(6223534104330821696)
XLA Ops:
  0.6 62.1 %shard_map.50 = (f32[8,64,256]{2,1,0:T(8,128)S(1)}, f32[4,128,256]{2,1,0:T(8,128)S(1)}) custom-call(f32[8,64,256]{2,1,0:T(8,128)} %u_hbm.1, f32[2,8,64,256]{3,2,1,0:T(8,128)} %e_hbm.1, f32[4,128,256]{2,1,0:T(8,128)} %cs_hbm.1), custom_call_target="tpu_custom_call" | custom-call | tf_op jit(solution)/shard_map/pallas_call | solution.py:293
  62.8 0.8 %copy.7 = f32[8,64,256]{2,1,0:T(8,128)} copy(f32[8,64,256]{2,1,0:T(8,128)S(1)} %get-tuple-element.2) | data formatting | bytes 1048576
  63.6 0.8 %copy.8 = f32[4,128,256]{2,1,0:T(8,128)} copy(f32[4,128,256]{2,1,0:T(8,128)S(1)} %get-tuple-element.3) | data formatting | bytes 1048576

commit v2 on v1

v2 whole, which is shorter than its diff:
```python
import functools

import jax
import jax.numpy as jnp
from jax import lax
from jax.experimental import pallas as pl
from jax.experimental.pallas import tpu as pltpu
from jax.sharding import PartitionSpec as P

MESH = pl.DeviceIdType.MESH
NOISE = 0.3
FINE_STEP = 0.2
COARSE_STEP = 0.4
COARSE_COUPLING = 0.5
S = 1.0 / 7.0
COARSE_SCALE = 1.0 / 4.0


def reaction(state, forcing, step):
    return state + step * (state - state * state * state) + NOISE * forcing


def ring_sum(center):
    rows, lanes = center.shape
    beside = pltpu.roll(center, rows - 1, 0) + pltpu.roll(center, 1, 0)
    return beside + (pltpu.roll(center, lanes - 1, 1) + pltpu.roll(center, 1, 1))


def kernel(sizes, u_hbm, e_hbm, cs_hbm, fo, co, u, e, cs, v1, v2, w, p0, k0, k1, zs1, zs2, pks, pkr,
           sums, c, cw, cblk, load_sem, send_sem, recv_sem):
    n_gx, n_gy, n_gz = sizes
    X, Y, Z = u.shape
    CX, CY, CZ = cs.shape
    me_x, me_y, me_z = lax.axis_index("gx"), lax.axis_index("gy"), lax.axis_index("gz")
    R, L = lax.rem(me_x + 1, n_gx), lax.rem(me_x + n_gx - 1, n_gx)
    U, D = lax.rem(me_y + 1, n_gy), lax.rem(me_y + n_gy - 1, n_gy)
    O = lax.rem(me_y + 2, n_gy)
    Q = lax.rem(me_z + 1, n_gz)
    one, zero, near, far = (0, X - 3), (X - 2, X - 1), (X, X + 1), (X + 2, X + 3)
    two = (1, X - 4)
    place = {0: X - 2, X - 1: X - 1}
    place.update({x: x - 1 for x in range(1, X - 1)})
    rows, lanes = slice(0, Y), slice(0, Z)

    def dev(x=None, y=None, z=None):
        return {"gx": me_x if x is None else x, "gy": me_y if y is None else y,
                "gz": me_z if z is None else z}

    loads = []

    def load(src, dst):
        copy = pltpu.make_async_copy(src, dst, load_sem.at[len(loads)])
        copy.start()
        loads.append(copy)
        return copy

    own_y = pl.ds(pl.multiple_of(me_y * CY, 8), CY)
    own_z = pl.ds(pl.multiple_of(me_z * CZ, 128), CZ)
    first = [load(u_hbm.at[0:2], u.at[0:2]), load(e_hbm.at[0, 0:2], e.at[0, 0:2]),
             load(u_hbm.at[X - 2 : X], u.at[X - 2 : X]),
             load(e_hbm.at[0, X - 2 : X], e.at[0, X - 2 : X])]
    second = [load(e_hbm.at[1], e.at[1]), load(e_hbm.at[0, 2 : X - 2], e.at[0, 2 : X - 2]),
              load(cs_hbm.at[:, own_y, own_z], cs)]
    third = load(u_hbm.at[2 : X - 2], u.at[2 : X - 2])

    barrier = pltpu.get_barrier_semaphore()
    partners = [dev(x=R, y=U), dev(x=R, y=D), dev(x=L, y=U), dev(x=L, y=D), dev(y=O),
                dev(x=R, z=Q), dev(x=L, z=Q), dev(x=R), dev(x=L),
                dev(y=U, z=Q), dev(y=D, z=Q), dev(y=U), dev(y=D), dev(z=Q)]
    for partner in partners:
        pl.semaphore_signal(barrier, inc=1, device_id=partner, device_id_type=MESH)

    sends = []

    def send(src, dst, to):
        k = len(sends)
        copy = pltpu.make_async_remote_copy(
            src_ref=src, dst_ref=dst, send_sem=send_sem.at[k], recv_sem=recv_sem.at[k],
            device_id=to, device_id_type=MESH)
        copy.start()
        sends.append(copy)
        return copy

    def wait(copies):
        for copy in copies:
            copy.wait_recv()

    def planes(start, stop, step_body):
        def step(k, carry):
            step_body(k)
            return carry
        lax.fori_loop(start, stop, step, 0)

    lane = lax.broadcasted_iota(jnp.int32, (Y, 128), 1)
    coarse_lane = lax.broadcasted_iota(jnp.int32, (CY, 128), 1)

    def first_advance(x, at):
        v1[at, rows, lanes] = reaction(u[x], e[0, x], FINE_STEP)

    def z_select(v, zs, k):
        zs[k] = jnp.where(lane < 64, v[k, rows, 0:128], v[k, rows, Z - 128 : Z])

    def pack(v, slot):
        columns = [jnp.where(lane == 0, v[k, rows, 0:128], pltpu.roll(v[k, rows, Z - 128 : Z], 8, 1))
                   for k in zero]
        pks[slot] = jnp.transpose(jnp.concatenate(columns, axis=0))[0:8, :]

    def unpacked(slot, side):
        return jnp.transpose(jnp.concatenate([pkr[slot, side]] * 16, axis=0))

    def unpack(v, slot):
        v[near[0], rows, Z : Z + 128] = unpacked(slot, 0)[Y : 2 * Y, :]
        v[near[1], rows, Z : Z + 128] = unpacked(slot, 1)[0:Y, :]

    def send_near(v):
        return [send(v.at[zero[1], rows, lanes], v.at[near[0], rows, lanes], dev(x=R)),
                send(v.at[zero[0], rows, lanes], v.at[near[1], rows, lanes], dev(x=L))]

    def send_far(v):
        return [send(v.at[one[1], rows, lanes], v.at[far[0], rows, lanes], dev(x=R)),
                send(v.at[one[0], rows, lanes], v.at[far[1], rows, lanes], dev(x=L))]

    def send_corner_rows(v):
        out = []
        for mine, theirs, x in ((zero[1], near[0], R), (zero[0], near[1], L)):
            out.append(send(v.at[mine, Y - 1 : Y, lanes], v.at[theirs, Y + 7 : Y + 8, lanes], dev(x=x, y=U)))
            out.append(send(v.at[mine, 0:1, lanes], v.at[theirs, Y : Y + 1, lanes], dev(x=x, y=D)))
        return out

    def send_packed(slot):
        return [send(pks.at[slot], pkr.at[slot, 0], dev(x=R, z=Q)),
                send(pks.at[slot], pkr.at[slot, 1], dev(x=L, z=Q))]

    def send_sides(v, zs, start, stop):
        ks = slice(start, stop)
        ring = slice(Z, Z + 128)
        return [
            send(v.at[ks, Y - 2 : Y, lanes], v.at[ks, Y + 6 : Y + 8, lanes], dev(y=U)),
            send(v.at[ks, 0:2, lanes], v.at[ks, Y : Y + 2, lanes], dev(y=D)),
            send(zs.at[ks, Y - 2 : Y], v.at[ks, Y + 6 : Y + 8, ring], dev(y=U, z=Q)),
            send(zs.at[ks, 0:2], v.at[ks, Y : Y + 2, ring], dev(y=D, z=Q)),
            send(zs.at[ks], v.at[ks, rows, ring], dev(z=Q)),
        ]

    def sweep_one(v, k, below, above):
        center = v[k]
        w[k] = (center + (v[above] + v[below] + ring_sum(center))) * S

    def partial_two(v, k, above):
        return v[k, rows, lanes] + (w[above, rows, lanes] + ring_sum(w[k])[rows, lanes])

    def sweep_two(v, k, below, above):
        return (partial_two(v, k, above) + w[below, rows, lanes]) * S

    for copy in first:
        copy.wait()
    for x in (0, X - 1, 1, X - 2):
        first_advance(x, place[x])
    for copy in second:
        copy.wait()
    for x in range(CX):
        total = (e[0, 2 * x] + e[0, 2 * x + 1]) + (e[1, 2 * x] + e[1, 2 * x + 1])
        for t in range(Z // 128):
            sums[t, x * Y : (x + 1) * Y, :] = total[:, t * 128 : (t + 1) * 128]
    pairs = [sums[t, pl.ds(0, CX * CY, stride=2), :] + sums[t, pl.ds(1, CX * CY, stride=2), :]
             for t in range(Z // 128)]
    halve = (lax.broadcasted_iota(jnp.int32, (Z, CZ), 0) // 2
             == lax.broadcasted_iota(jnp.int32, (Z, CZ), 1)).astype(jnp.float32)
    noise = 0.125 * jnp.dot(jnp.concatenate(pairs, axis=1), halve,
                            precision=lax.Precision.HIGHEST, preferred_element_type=jnp.float32)
    c[2 : CX + 2, 0:CY, 0:CZ] = reaction(cs[...], noise.reshape(CX, CY, CZ), COARSE_STEP)
    columns = [jnp.where(coarse_lane == 0, c[k, 0:CY, 0:CZ], pltpu.roll(c[k, 0:CY, 0:CZ], 8, 1))
               for k in (2, CX + 1)]
    pks[2] = jnp.transpose(jnp.concatenate(columns * 2, axis=0))[0:8, :]
    pack(v1, 0)

    pl.semaphore_wait(barrier, len(partners))
    inner = slice(2, CX + 2)
    coarse = []
    for mine, theirs, x in ((CX + 1, 1, R), (2, CX + 2, L)):
        coarse.append(send(c.at[mine, CY - 1 : CY, 0:CZ], c.at[theirs, CY + 7 : CY + 8, 0:CZ], dev(x=x, y=U)))
        coarse.append(send(c.at[mine, 0:1, 0:CZ], c.at[theirs, CY : CY + 1, 0:CZ], dev(x=x, y=D)))
    coarse += [
        send(c.at[CX : CX + 2, 0:CY, 0:CZ], c.at[0:2, 0:CY, 0:CZ], dev(x=R)),
        send(c.at[2:4, 0:CY, 0:CZ], c.at[CX + 2 : CX + 4, 0:CY, 0:CZ], dev(x=L)),
    ]
    coarse += send_packed(2)
    near1 = send_near(v1)
    corner1 = send_corner_rows(v1) + send_packed(0)
    far1 = send_far(v1)
    coarse += [
        send(c.at[inner, CY - 2 : CY, 0:CZ], c.at[inner, CY + 6 : CY + 8, 0:CZ], dev(y=U)),
        send(c.at[inner, 0:2, 0:CZ], c.at[inner, CY : CY + 2, 0:CZ], dev(y=D)),
        send(c.at[inner, CY - 1 : CY, 0:CZ], c.at[inner, CY + 7 : CY + 8, CZ : 2 * CZ], dev(y=U, z=Q)),
        send(c.at[inner, 0:1, 0:CZ], c.at[inner, CY : CY + 1, CZ : 2 * CZ], dev(y=D, z=Q)),
        send(c.at[inner, 0:CY, 0:CZ], c.at[inner, 0:CY, CZ : 2 * CZ], dev(z=Q)),
    ]
    third.wait()
    planes(2, X - 2, lambda x: first_advance(x, x - 1))
    planes(0, X, lambda k: z_select(v1, zs1, k))
    sides1 = send_sides(v1, zs1, 0, X)

    wait(sides1)
    planes(1, X - 3, lambda k: sweep_one(v1, k, k - 1, k + 1))
    for s in range(2):
        sweep_one(v1, one[s], zero[s], two[s])
        center = v1[zero[s]]
        p0[s] = center + (v1[one[s]] + ring_sum(center))
    for s in range(2):
        k1[s] = partial_two(v1, one[s], two[s])

    def second_advance(k):
        v2[k, rows, lanes] = reaction(sweep_two(v1, k, k - 1, k + 1), e[1, k + 1], FINE_STEP)

    planes(1, X - 3, second_advance)

    wait(coarse)
    c[1, 0:CY, CZ : 2 * CZ] = unpacked(2, 0)[CY : 2 * CY, :]
    c[CX + 2, 0:CY, CZ : 2 * CZ] = unpacked(2, 1)[0:CY, :]
    for k in range(1, CX + 3):
        center = c[k]
        beside = c[k + 1] + c[k - 1] + ring_sum(center)
        cw[k - 1] = (center + COARSE_COUPLING * beside) * COARSE_SCALE
    for k in range(2, CX + 2):
        beside = cw[k, 0:CY, 0:CZ] + cw[k - 2, 0:CY, 0:CZ] + ring_sum(cw[k - 1])[0:CY, 0:CZ]
        cblk[k - 2] = (c[k, 0:CY, 0:CZ] + COARSE_COUPLING * beside) * COARSE_SCALE
    mine = co.at[:, own_y, own_z]
    gather = [send(cblk, mine, dev(y=O)), send(cblk, mine, dev(y=U)), send(cblk, mine, dev(y=D))]
    direct = send(cblk, mine, dev(z=Q))
    co[:, own_y, own_z] = cblk[...]

    ends = (0, X - 1)
    nexts = (1, X - 2)
    wait(near1)
    for s in range(2):
        outer = (p0[s, rows, lanes] + v1[near[s], rows, lanes]) * S
        v2[one[s], rows, lanes] = reaction((k1[s] + outer) * S, e[1, nexts[s]], FINE_STEP)
    far2 = send_far(v2)
    planes(0, X - 2, lambda k: z_select(v2, zs2, k))
    inside2 = send_sides(v2, zs2, 0, X - 2)

    wait(corner1)
    unpack(v1, 0)
    for s in range(2):
        outside = v1[near[s]]
        w[zero[s]] = (p0[s] + outside) * S
        beyond = (outside + ring_sum(outside))[rows, lanes] + v1[zero[s], rows, lanes]
        k0[s] = partial_two(v1, zero[s], one[s]) + beyond * S
    wait(far1)
    for s in range(2):
        total = (k0[s] + v1[far[s], rows, lanes] * S) * S
        v2[zero[s], rows, lanes] = reaction(total, e[1, ends[s]], FINE_STEP)
    corner2 = send_corner_rows(v2)
    near2 = send_near(v2)
    pack(v2, 1)
    corner2 += send_packed(1)
    for k in zero:
        z_select(v2, zs2, k)
    outside2 = send_sides(v2, zs2, X - 2, X)

    wait(inside2)
    planes(1, X - 3, lambda k: sweep_one(v2, k, k - 1, k + 1))

    def finish(k):
        fo[k + 1] = sweep_two(v2, k, k - 1, k + 1)

    planes(2, X - 4, finish)

    passed = []

    def pass_on(copy, owner):
        copy.wait_recv()
        block = co.at[:, pl.ds(pl.multiple_of(owner * CY, 8), CY), own_z]
        passed.append(send(block, block, dev(z=Q)))

    pass_on(gather[1], D)
    pass_on(gather[2], U)

    wait(outside2)
    three = (2, X - 5)
    for s in range(2):
        sweep_one(v2, one[s], zero[s], two[s])
        center = v2[zero[s]]
        p0[s] = center + (v2[one[s]] + ring_sum(center))
    for s in range(2):
        fo[place_of(two[s], X)] = sweep_two(v2, two[s], one[s], three[s])
        k1[s] = partial_two(v2, one[s], two[s]) + p0[s, rows, lanes] * S
        k0[s] = (v2[zero[s], rows, lanes] + w[one[s], rows, lanes]
                 + (ring_sum(p0[s])[rows, lanes] + v2[zero[s], rows, lanes]) * S)
    pass_on(gather[0], O)
    wait(far2)
    for s in range(2):
        k0[s] = k0[s] + v2[far[s], rows, lanes] * S
    wait(corner2)
    unpack(v2, 1)
    wait(near2)
    for s in range(2):
        outside = v2[near[s]]
        middle = outside[rows, lanes]
        fo[nexts[s]] = (k1[s] + middle * S) * S
        fo[ends[s]] = (k0[s] + (2.0 * ring_sum(outside)[rows, lanes] + middle) * S) * S

    direct.wait_recv()
    wait(passed)
    for copy in sends:
        copy.wait_send()


def place_of(k, X):
    return k + 1


def write_out(fine, coarse, fine_hbm, coarse_hbm, sems):
    copies = []
    for src, dst in ((fine, fine_hbm), (coarse, coarse_hbm)):
        half = src.shape[0] // 2
        for k in range(2):
            part = slice(k * half, (k + 1) * half)
            copies.append(pltpu.make_async_copy(src.at[part], dst.at[part], sems.at[len(copies)]))
    for copy in copies:
        copy.start()
    for copy in copies:
        copy.wait()


N_MESSAGES = 64


def body(sizes, fine_start, increments, coarse_start):
    X, Y, Z = fine_start.shape
    CX, CY, CZ = X // 2, Y // 2, Z // 2
    f32 = jnp.float32
    any_space = pl.BlockSpec(memory_space=pl.ANY)
    in_vmem = pl.BlockSpec(memory_space=pltpu.VMEM)
    fine, coarse = pl.pallas_call(
        functools.partial(kernel, sizes),
        out_shape=(pltpu.VMEM((X, Y, Z), f32), pltpu.VMEM(coarse_start.shape, f32)),
        in_specs=[any_space] * 3,
        out_specs=(in_vmem, in_vmem),
        scratch_shapes=[
            pltpu.VMEM((X, Y, Z), f32),
            pltpu.VMEM((2, X, Y, Z), f32),
            pltpu.VMEM((CX, CY, CZ), f32),
            pltpu.VMEM((X + 4, Y + 8, Z + 128), f32),
            pltpu.VMEM((X + 4, Y + 8, Z + 128), f32),
            pltpu.VMEM((X, Y + 8, Z + 128), f32),
            pltpu.VMEM((2, Y + 8, Z + 128), f32),
            pltpu.VMEM((2, Y, Z), f32),
            pltpu.VMEM((2, Y, Z), f32),
            pltpu.VMEM((X, Y, 128), f32),
            pltpu.VMEM((X, Y, 128), f32),
            pltpu.VMEM((3, 8, 128), f32),
            pltpu.VMEM((3, 2, 8, 128), f32),
            pltpu.VMEM((Z // 128, CX * Y, 128), f32),
            pltpu.VMEM((CX + 4, CY + 8, 2 * CZ), f32),
            pltpu.VMEM((CX + 2, CY + 8, 2 * CZ), f32),
            pltpu.VMEM((CX, CY, CZ), f32),
            pltpu.SemaphoreType.DMA((8,)),
            pltpu.SemaphoreType.DMA((N_MESSAGES,)),
            pltpu.SemaphoreType.DMA((N_MESSAGES,)),
        ],
        compiler_params=pltpu.CompilerParams(collective_id=0, has_side_effects=True),
    )(fine_start, increments, coarse_start)
    fine = pltpu.with_memory_space_constraint(fine, pltpu.VMEM)
    coarse = pltpu.with_memory_space_constraint(coarse, pltpu.VMEM)
    return pl.pallas_call(
        write_out,
        out_shape=(jax.ShapeDtypeStruct(fine_start.shape, f32),
                   jax.ShapeDtypeStruct(coarse_start.shape, f32)),
        in_specs=[in_vmem, in_vmem],
        out_specs=(any_space, any_space),
        scratch_shapes=[pltpu.SemaphoreType.DMA((4,))],
    )(fine, coarse)


def solution(mesh):
    sizes = tuple(mesh.shape[name] for name in ("gx", "gy", "gz"))
    return jax.shard_map(
        functools.partial(body, sizes),
        mesh=mesh,
        in_specs=(
            P(("pairs", "gx"), "gy", "gz"),
            P(None, ("pairs", "gx"), "gy", "gz"),
            P(("pairs", "gx"), None, None),
        ),
        out_specs=(P(("pairs", "gx"), "gy", "gz"), P(("pairs", "gx"), None, None)),
        check_vma=False,
    )
```

time: 64.5 us -> 63.9 us (level)
  local copies, waits for them, and re-layouts: 1.59 us -> 0 us
  Pallas kernels: 62.1 us -> 63.1 us
    unnamed x2 -> x0, local copies, waits for them, and re-layouts: 1.59 us -> none
    pallas_call x0 -> x1, Pallas kernels: none -> 1 us  [body(): pl.pallas_call(write_out, out_shape=(jax.ShapeDtypeStruct(fine_start.shap...]
where the time goes in v2:
time: 63.9 us; the launch traced here: 63.8 us
  Pallas kernels  63.1 us (99%)
  between operations  0.64 us (1%)
    pallas_call x1, Pallas kernels, body(): pl.pallas_call(functools.partial(kernel, sizes), out_shape=(pltpu.VMEM((X...  62.1 us

profile of v2, /device:TPU:33, one launch (start us, length us, event | category | flops | bytes accessed | tf_op | source)
XLA Modules:
  0.0 63.8 jit_solution(5530261909584694184)
XLA Ops:
  0.6 62.1 %shard_map.50 = (f32[8,64,256]{2,1,0:T(8,128)S(1)}, f32[4,128,256]{2,1,0:T(8,128)S(1)}) custom-call(f32[8,64,256]{2,1,0:T(8,128)} %u_hbm.1, f32[2,8,64,256]{3,2,1,0:T(8,128)} %e_hbm.1, f32[4,128,256]{2,1,0:T(8,128)} %cs_hbm.1), custom_call_target="tpu_custom_call" | custom-call | tf_op jit(solution)/shard_map/pallas_call | solution.py:335
  62.8 1.0 %shard_map.51 = (f32[8,64,256]{2,1,0:T(8,128)}, f32[4,128,256]{2,1,0:T(8,128)}) custom-call(f32[8,64,256]{2,1,0:T(8,128)S(1)} %get-tuple-element.4.fine, f32[4,128,256]{2,1,0:T(8,128)S(1)} %get-tuple-element.5.coarse), custom_call_target="tpu_custom_call" | custom-call | tf_op jit(solution)/shard_map/pallas_call | solution.py:366

commit v3 on v2

--- a/solution.py
+++ b/solution.py
@@ -77,9 +77,14 @@
         copy = pltpu.make_async_remote_copy(
             src_ref=src, dst_ref=dst, send_sem=send_sem.at[k], recv_sem=recv_sem.at[k],
             device_id=to, device_id_type=MESH)
-        copy.start()
         sends.append(copy)
         return copy
+
+    def start(*groups):
+        for group in groups:
+            for copy in group:
+                copy.start()
+        return groups[0]
 
     def wait(copies):
         for copy in copies:
@@ -176,45 +181,36 @@
 
     pl.semaphore_wait(barrier, len(partners))
     inner = slice(2, CX + 2)
-    coarse = []
+    coarse_x = []
     for mine, theirs, x in ((CX + 1, 1, R), (2, CX + 2, L)):
-        coarse.append(send(c.at[mine, CY - 1 : CY, 0:CZ], c.at[theirs, CY + 7 : CY + 8, 0:CZ], dev(x=x, y=U)))
-        coarse.append(send(c.at[mine, 0:1, 0:CZ], c.at[theirs, CY : CY + 1, 0:CZ], dev(x=x, y=D)))
-    coarse += [
+        coarse_x.append(send(c.at[mine, CY - 1 : CY, 0:CZ], c.at[theirs, CY + 7 : CY + 8, 0:CZ], dev(x=x, y=U)))
+        coarse_x.append(send(c.at[mine, 0:1, 0:CZ], c.at[theirs, CY : CY + 1, 0:CZ], dev(x=x, y=D)))
+    coarse_x += [
         send(c.at[CX : CX + 2, 0:CY, 0:CZ], c.at[0:2, 0:CY, 0:CZ], dev(x=R)),
         send(c.at[2:4, 0:CY, 0:CZ], c.at[CX + 2 : CX + 4, 0:CY, 0:CZ], dev(x=L)),
     ]
-    coarse += send_packed(2)
-    near1 = send_near(v1)
-    corner1 = send_corner_rows(v1) + send_packed(0)
-    far1 = send_far(v1)
-    coarse += [
+    coarse_x += send_packed(2)
+    coarse_yz = [
         send(c.at[inner, CY - 2 : CY, 0:CZ], c.at[inner, CY + 6 : CY + 8, 0:CZ], dev(y=U)),
         send(c.at[inner, 0:2, 0:CZ], c.at[inner, CY : CY + 2, 0:CZ], dev(y=D)),
         send(c.at[inner, CY - 1 : CY, 0:CZ], c.at[inner, CY + 7 : CY + 8, CZ : 2 * CZ], dev(y=U, z=Q)),
         send(c.at[inner, 0:1, 0:CZ], c.at[inner, CY : CY + 1, CZ : 2 * CZ], dev(y=D, z=Q)),
         send(c.at[inner, 0:CY, 0:CZ], c.at[inner, 0:CY, CZ : 2 * CZ], dev(z=Q)),
     ]
+    near1 = send_near(v1)
+    corner1 = send_corner_rows(v1) + send_packed(0)
+    far1 = send_far(v1)
+    sides1 = send_sides(v1, zs1, 0, X)
+    start(coarse_x, near1, corner1, far1, coarse_yz)
     third.wait()
     planes(2, X - 2, lambda x: first_advance(x, x - 1))
     planes(0, X, lambda k: z_select(v1, zs1, k))
-    sides1 = send_sides(v1, zs1, 0, X)
+    start(sides1)
 
     wait(sides1)
     planes(1, X - 3, lambda k: sweep_one(v1, k, k - 1, k + 1))
-    for s in range(2):
-        sweep_one(v1, one[s], zero[s], two[s])
-        center = v1[zero[s]]
-        p0[s] = center + (v1[one[s]] + ring_sum(center))
-    for s in range(2):
-        k1[s] = partial_two(v1, one[s], two[s])
-
-    def second_advance(k):
-        v2[k, rows, lanes] = reaction(sweep_two(v1, k, k - 1, k + 1), e[1, k + 1], FINE_STEP)
-
-    planes(1, X - 3, second_advance)
-
-    wait(coarse)
+    wait(coarse_yz)
+    wait(coarse_x)
     c[1, 0:CY, CZ : 2 * CZ] = unpacked(2, 0)[CY : 2 * CY, :]
     c[CX + 2, 0:CY, CZ : 2 * CZ] = unpacked(2, 1)[0:CY, :]
     for k in range(1, CX + 3):
@@ -227,7 +223,22 @@
     mine = co.at[:, own_y, own_z]
     gather = [send(cblk, mine, dev(y=O)), send(cblk, mine, dev(y=U)), send(cblk, mine, dev(y=D))]
     direct = send(cblk, mine, dev(z=Q))
+
+    start(gather)
+    direct.start()
     co[:, own_y, own_z] = cblk[...]
+
+    for s in range(2):
+        sweep_one(v1, one[s], zero[s], two[s])
+        center = v1[zero[s]]
+        p0[s] = center + (v1[one[s]] + ring_sum(center))
+    for s in range(2):
+        k1[s] = partial_two(v1, one[s], two[s])
+
+    def second_advance(k):
+        v2[k, rows, lanes] = reaction(sweep_two(v1, k, k - 1, k + 1), e[1, k + 1], FINE_STEP)
+
+    planes(1, X - 3, second_advance)
 
     ends = (0, X - 1)
     nexts = (1, X - 2)
@@ -235,9 +246,10 @@
     for s in range(2):
         outer = (p0[s, rows, lanes] + v1[near[s], rows, lanes]) * S
         v2[one[s], rows, lanes] = reaction((k1[s] + outer) * S, e[1, nexts[s]], FINE_STEP)
-    far2 = send_far(v2)
+    far2 = start(send_far(v2))
     planes(0, X - 2, lambda k: z_select(v2, zs2, k))
-    inside2 = send_sides(v2, zs2, 0, X - 2)
+    inside2 = start(send_sides(v2, zs2, 0, X - 2))
+
 
     wait(corner1)
     unpack(v1, 0)
@@ -250,13 +262,13 @@
     for s in range(2):
         total = (k0[s] + v1[far[s], rows, lanes] * S) * S
         v2[zero[s], rows, lanes] = reaction(total, e[1, ends[s]], FINE_STEP)
-    corner2 = send_corner_rows(v2)
-    near2 = send_near(v2)
+    corner2 = start(send_corner_rows(v2))
+    near2 = start(send_near(v2))
     pack(v2, 1)
-    corner2 += send_packed(1)
+    corner2 = corner2 + start(send_packed(1))
     for k in zero:
         z_select(v2, zs2, k)
-    outside2 = send_sides(v2, zs2, X - 2, X)
+    outside2 = start(send_sides(v2, zs2, X - 2, X))
 
     wait(inside2)
     planes(1, X - 3, lambda k: sweep_one(v2, k, k - 1, k + 1))
@@ -272,6 +284,7 @@
         copy.wait_recv()
         block = co.at[:, pl.ds(pl.multiple_of(owner * CY, 8), CY), own_z]
         passed.append(send(block, block, dev(z=Q)))
+        passed[-1].start()
 
     pass_on(gather[1], D)
     pass_on(gather[2], U)

time: 63.9 us -> 63 us (0.986)
  Pallas kernels: 63.1 us -> 62.2 us
    pallas_call x1, Pallas kernels: 62.1 us -> 61.2 us  [body(): pl.pallas_call(functools.partial(kernel, sizes), out_shape=(pltpu.VMEM((X...]
where the time goes in v3:
time: 63 us; the launch traced here: 62.8 us
  Pallas kernels  62.2 us (99%)
  between operations  0.64 us (1%)
    pallas_call x1, Pallas kernels, body(): pl.pallas_call(functools.partial(kernel, sizes), out_shape=(pltpu.VMEM((X...  61.2 us

profile of v3, /device:TPU:33, one launch (start us, length us, event | category | flops | bytes accessed | tf_op | source)
XLA Modules:
  0.0 62.8 jit_solution(13913628089644986095)
XLA Ops:
  0.6 61.2 %shard_map.50 = (f32[8,64,256]{2,1,0:T(8,128)S(1)}, f32[4,128,256]{2,1,0:T(8,128)S(1)}) custom-call(f32[8,64,256]{2,1,0:T(8,128)} %u_hbm.1, f32[2,8,64,256]{3,2,1,0:T(8,128)} %e_hbm.1, f32[4,128,256]{2,1,0:T(8,128)} %cs_hbm.1), custom_call_target="tpu_custom_call" | custom-call | tf_op jit(solution)/shard_map/pallas_call | solution.py:348
  61.8 1.0 %shard_map.51 = (f32[8,64,256]{2,1,0:T(8,128)}, f32[4,128,256]{2,1,0:T(8,128)}) custom-call(f32[8,64,256]{2,1,0:T(8,128)S(1)} %get-tuple-element.4.fine, f32[4,128,256]{2,1,0:T(8,128)S(1)} %get-tuple-element.5.coarse), custom_call_target="tpu_custom_call" | custom-call | tf_op jit(solution)/shard_map/pallas_call | solution.py:379

commit v4 on v3

--- a/solution.py
+++ b/solution.py
@@ -36,10 +36,10 @@
     U, D = lax.rem(me_y + 1, n_gy), lax.rem(me_y + n_gy - 1, n_gy)
     O = lax.rem(me_y + 2, n_gy)
     Q = lax.rem(me_z + 1, n_gz)
-    one, zero, near, far = (0, X - 3), (X - 2, X - 1), (X, X + 1), (X + 2, X + 3)
-    two = (1, X - 4)
-    place = {0: X - 2, X - 1: X - 1}
-    place.update({x: x - 1 for x in range(1, X - 1)})
+    one, zero, near, far = (X - 4, X - 3), (X - 2, X - 1), (X, X + 1), (X + 2, X + 3)
+    two, three = (0, X - 5), (1, X - 6)
+    place = {1: X - 4, X - 2: X - 3, 0: X - 2, X - 1: X - 1}
+    place.update({x: x - 2 for x in range(2, X - 2)})
     rows, lanes = slice(0, Y), slice(0, Z)
 
     def dev(x=None, y=None, z=None):
@@ -53,15 +53,6 @@
         copy.start()
         loads.append(copy)
         return copy
-
-    own_y = pl.ds(pl.multiple_of(me_y * CY, 8), CY)
-    own_z = pl.ds(pl.multiple_of(me_z * CZ, 128), CZ)
-    first = [load(u_hbm.at[0:2], u.at[0:2]), load(e_hbm.at[0, 0:2], e.at[0, 0:2]),
-             load(u_hbm.at[X - 2 : X], u.at[X - 2 : X]),
-             load(e_hbm.at[0, X - 2 : X], e.at[0, X - 2 : X])]
-    second = [load(e_hbm.at[1], e.at[1]), load(e_hbm.at[0, 2 : X - 2], e.at[0, 2 : X - 2]),
-              load(cs_hbm.at[:, own_y, own_z], cs)]
-    third = load(u_hbm.at[2 : X - 2], u.at[2 : X - 2])
 
     barrier = pltpu.get_barrier_semaphore()
     partners = [dev(x=R, y=U), dev(x=R, y=D), dev(x=L, y=U), dev(x=L, y=D), dev(y=O),
@@ -69,6 +60,13 @@
                 dev(y=U, z=Q), dev(y=D, z=Q), dev(y=U), dev(y=D), dev(z=Q)]
     for partner in partners:
         pl.semaphore_signal(barrier, inc=1, device_id=partner, device_id_type=MESH)
+
+    own_y = pl.ds(pl.multiple_of(me_y * CY, 8), CY)
+    own_z = pl.ds(pl.multiple_of(me_z * CZ, 128), CZ)
+    first = [load(e_hbm.at[0], e.at[0]), load(e_hbm.at[1], e.at[1]),
+             load(cs_hbm.at[:, own_y, own_z], cs)]
+    second = [load(u_hbm.at[0:2], u.at[0:2]), load(u_hbm.at[X - 2 : X], u.at[X - 2 : X])]
+    third = load(u_hbm.at[2 : X - 2], u.at[2 : X - 2])
 
     sends = []
 
@@ -117,20 +115,28 @@
         v[near[0], rows, Z : Z + 128] = unpacked(slot, 0)[Y : 2 * Y, :]
         v[near[1], rows, Z : Z + 128] = unpacked(slot, 1)[0:Y, :]
 
-    def send_near(v):
-        return [send(v.at[zero[1], rows, lanes], v.at[near[0], rows, lanes], dev(x=R)),
-                send(v.at[zero[0], rows, lanes], v.at[near[1], rows, lanes], dev(x=L))]
-
-    def send_far(v):
-        return [send(v.at[one[1], rows, lanes], v.at[far[0], rows, lanes], dev(x=R)),
-                send(v.at[one[0], rows, lanes], v.at[far[1], rows, lanes], dev(x=L))]
-
-    def send_corner_rows(v):
-        out = []
-        for mine, theirs, x in ((zero[1], near[0], R), (zero[0], near[1], L)):
-            out.append(send(v.at[mine, Y - 1 : Y, lanes], v.at[theirs, Y + 7 : Y + 8, lanes], dev(x=x, y=U)))
-            out.append(send(v.at[mine, 0:1, lanes], v.at[theirs, Y : Y + 1, lanes], dev(x=x, y=D)))
-        return out
+    def send_near(v, part):
+        return [send(v.at[zero[1], part, lanes], v.at[near[0], part, lanes], dev(x=R)),
+                send(v.at[zero[0], part, lanes], v.at[near[1], part, lanes], dev(x=L))]
+
+    def send_far(v, part):
+        return [send(v.at[one[1], part, lanes], v.at[far[0], part, lanes], dev(x=R)),
+                send(v.at[one[0], part, lanes], v.at[far[1], part, lanes], dev(x=L))]
+
+    def send_corner_rows(v, half):
+        mine, theirs, y = ((0, Y, D), (Y - 1, Y + 7, U))[half]
+        return [
+            send(v.at[zero[1], mine : mine + 1, lanes], v.at[near[0], theirs : theirs + 1, lanes], dev(x=R, y=y)),
+            send(v.at[zero[0], mine : mine + 1, lanes], v.at[near[1], theirs : theirs + 1, lanes], dev(x=L, y=y)),
+        ]
+
+    M = Y // 2
+    halves = (slice(0, M), slice(M, Y))
+
+    def widened(ref, k, half):
+        if half:
+            return ref[k, M - 8 : Y + 8, :]
+        return jnp.concatenate([ref[k, Y : Y + 8, :], ref[k, 0 : M + 8, :]], axis=0)
 
     def send_packed(slot):
         return [send(pks.at[slot], pkr.at[slot, 0], dev(x=R, z=Q)),
@@ -158,10 +164,6 @@
         return (partial_two(v, k, above) + w[below, rows, lanes]) * S
 
     for copy in first:
-        copy.wait()
-    for x in (0, X - 1, 1, X - 2):
-        first_advance(x, place[x])
-    for copy in second:
         copy.wait()
     for x in range(CX):
         total = (e[0, 2 * x] + e[0, 2 * x + 1]) + (e[1, 2 * x] + e[1, 2 * x + 1])
@@ -177,8 +179,11 @@
     columns = [jnp.where(coarse_lane == 0, c[k, 0:CY, 0:CZ], pltpu.roll(c[k, 0:CY, 0:CZ], 8, 1))
                for k in (2, CX + 1)]
     pks[2] = jnp.transpose(jnp.concatenate(columns * 2, axis=0))[0:8, :]
+    for copy in second:
+        copy.wait()
+    for x in (0, X - 1, 1, X - 2):
+        first_advance(x, place[x])
     pack(v1, 0)
-
     pl.semaphore_wait(barrier, len(partners))
     inner = slice(2, CX + 2)
     coarse_x = []
@@ -197,29 +202,41 @@
         send(c.at[inner, 0:1, 0:CZ], c.at[inner, CY : CY + 1, CZ : 2 * CZ], dev(y=D, z=Q)),
         send(c.at[inner, 0:CY, 0:CZ], c.at[inner, 0:CY, CZ : 2 * CZ], dev(z=Q)),
     ]
-    near1 = send_near(v1)
-    corner1 = send_corner_rows(v1) + send_packed(0)
-    far1 = send_far(v1)
+    near1 = [send_near(v1, slice(0, M + 8)), send_near(v1, slice(M + 8, Y))]
+    corner1 = send_corner_rows(v1, 0) + send_corner_rows(v1, 1) + send_packed(0)
+    far1 = [send_far(v1, half) for half in halves]
     sides1 = send_sides(v1, zs1, 0, X)
-    start(coarse_x, near1, corner1, far1, coarse_yz)
+    start(coarse_x, near1[0], corner1, far1[0], near1[1], far1[1], coarse_yz)
     third.wait()
-    planes(2, X - 2, lambda x: first_advance(x, x - 1))
+    planes(2, X - 2, lambda x: first_advance(x, x - 2))
     planes(0, X, lambda k: z_select(v1, zs1, k))
     start(sides1)
 
-    wait(sides1)
-    planes(1, X - 3, lambda k: sweep_one(v1, k, k - 1, k + 1))
+    H, G = COARSE_COUPLING, COARSE_SCALE
+    own = (slice(0, CY), slice(0, CZ))
+    ends_c, nexts_c, near_c, far_c = (2, CX + 1), (3, CX), (1, CX + 2), (0, CX + 3)
     wait(coarse_yz)
+    for k in range(3, CX + 1):
+        cw[k] = (c[k] + H * (c[k + 1] + c[k - 1] + ring_sum(c[k]))) * G
+    kept = []
+    for s in range(2):
+        end, inside = ends_c[s], nexts_c[s]
+        part = c[end] + H * (c[inside] + ring_sum(c[end]))
+        inner_one = cw[inside]
+        beyond = cw[nexts_c[1 - s], 0:CY, 0:CZ]
+        next_sum = c[inside, 0:CY, 0:CZ] + H * (ring_sum(inner_one)[own] + beyond + G * part[own])
+        end_sum = c[end, 0:CY, 0:CZ] + H * (inner_one[own] + G * (ring_sum(part)[own] + H * c[end, 0:CY, 0:CZ]))
+        kept.append((next_sum, end_sum))
     wait(coarse_x)
-    c[1, 0:CY, CZ : 2 * CZ] = unpacked(2, 0)[CY : 2 * CY, :]
-    c[CX + 2, 0:CY, CZ : 2 * CZ] = unpacked(2, 1)[0:CY, :]
-    for k in range(1, CX + 3):
-        center = c[k]
-        beside = c[k + 1] + c[k - 1] + ring_sum(center)
-        cw[k - 1] = (center + COARSE_COUPLING * beside) * COARSE_SCALE
-    for k in range(2, CX + 2):
-        beside = cw[k, 0:CY, 0:CZ] + cw[k - 2, 0:CY, 0:CZ] + ring_sum(cw[k - 1])[0:CY, 0:CZ]
-        cblk[k - 2] = (c[k, 0:CY, 0:CZ] + COARSE_COUPLING * beside) * COARSE_SCALE
+    for s in range(2):
+        c[near_c[s], 0:CY, CZ : 2 * CZ] = unpacked(2, s)[(1 - s) * CY : (2 - s) * CY, :]
+    for s in range(2):
+        outside = c[near_c[s]]
+        middle = outside[own]
+        next_sum, end_sum = kept[s]
+        cblk[nexts_c[s] - 2] = (next_sum + (H * H * G) * middle) * G
+        spread = 2.0 * H * ring_sum(outside)[own] + middle + H * c[far_c[s], 0:CY, 0:CZ]
+        cblk[ends_c[s] - 2] = (end_sum + (H * G) * spread) * G
     mine = co.at[:, own_y, own_z]
     gather = [send(cblk, mine, dev(y=O)), send(cblk, mine, dev(y=U)), send(cblk, mine, dev(y=D))]
     direct = send(cblk, mine, dev(z=Q))
@@ -228,6 +245,9 @@
     direct.start()
     co[:, own_y, own_z] = cblk[...]
 
+    wait(sides1)
+    for x in range(2, X - 2):
+        sweep_one(v1, place[x], place[x - 1], place[x + 1])
     for s in range(2):
         sweep_one(v1, one[s], zero[s], two[s])
         center = v1[zero[s]]
@@ -235,48 +255,53 @@
     for s in range(2):
         k1[s] = partial_two(v1, one[s], two[s])
 
-    def second_advance(k):
-        v2[k, rows, lanes] = reaction(sweep_two(v1, k, k - 1, k + 1), e[1, k + 1], FINE_STEP)
-
-    planes(1, X - 3, second_advance)
+    for x in range(2, X - 2):
+        total = sweep_two(v1, place[x], place[x - 1], place[x + 1])
+        v2[place[x], rows, lanes] = reaction(total, e[1, x], FINE_STEP)
+    planes(0, X - 4, lambda k: z_select(v2, zs2, k))
+    inside2 = start(send_sides(v2, zs2, 0, X - 4))
 
     ends = (0, X - 1)
     nexts = (1, X - 2)
-    wait(near1)
-    for s in range(2):
-        outer = (p0[s, rows, lanes] + v1[near[s], rows, lanes]) * S
-        v2[one[s], rows, lanes] = reaction((k1[s] + outer) * S, e[1, nexts[s]], FINE_STEP)
-    far2 = start(send_far(v2))
-    planes(0, X - 2, lambda k: z_select(v2, zs2, k))
-    inside2 = start(send_sides(v2, zs2, 0, X - 2))
-
-
-    wait(corner1)
-    unpack(v1, 0)
-    for s in range(2):
-        outside = v1[near[s]]
-        w[zero[s]] = (p0[s] + outside) * S
-        beyond = (outside + ring_sum(outside))[rows, lanes] + v1[zero[s], rows, lanes]
-        k0[s] = partial_two(v1, zero[s], one[s]) + beyond * S
-    wait(far1)
-    for s in range(2):
-        total = (k0[s] + v1[far[s], rows, lanes] * S) * S
-        v2[zero[s], rows, lanes] = reaction(total, e[1, ends[s]], FINE_STEP)
-    corner2 = start(send_corner_rows(v2))
-    near2 = start(send_near(v2))
+    early = list(sends)
+    far2, near2, corner2 = [], [], []
+    for half in range(2):
+        part = halves[half]
+        wait(near1[half])
+        for s in range(2):
+            outer = (p0[s, part, lanes] + v1[near[s], part, lanes]) * S
+            v2[one[s], part, lanes] = reaction((k1[s, part] + outer) * S, e[1, nexts[s], part], FINE_STEP)
+        far2 += start(send_far(v2, part))
+        if half == 0:
+            wait(corner1)
+            unpack(v1, 0)
+        for s in range(2):
+            outside = widened(v1, near[s], half)
+            first_sweep = (widened(p0, s, half) + outside) * S
+            beyond = (outside + ring_sum(outside))[8 : M + 8, lanes] + v1[zero[s], part, lanes]
+            within = w[one[s], part, lanes] + ring_sum(first_sweep)[8 : M + 8, lanes]
+            k0[s, part] = v1[zero[s], part, lanes] + within + beyond * S
+        wait(far1[half])
+        for s in range(2):
+            total = (k0[s, part] + v1[far[s], part, lanes] * S) * S
+            v2[zero[s], part, lanes] = reaction(total, e[1, ends[s], part], FINE_STEP)
+        corner2 += start(send_corner_rows(v2, half))
+        near2 += start(send_near(v2, part))
     pack(v2, 1)
-    corner2 = corner2 + start(send_packed(1))
-    for k in zero:
-        z_select(v2, zs2, k)
-    outside2 = start(send_sides(v2, zs2, X - 2, X))
+    corner2 += start(send_packed(1))
+    planes(X - 4, X, lambda k: z_select(v2, zs2, k))
+    outside2 = start(send_sides(v2, zs2, X - 4, X))
 
     wait(inside2)
-    planes(1, X - 3, lambda k: sweep_one(v2, k, k - 1, k + 1))
-
-    def finish(k):
-        fo[k + 1] = sweep_two(v2, k, k - 1, k + 1)
-
-    planes(2, X - 4, finish)
+    for s in range(2):
+        k = two[s]
+        beside = v2[one[s], rows, lanes] + v2[three[s], rows, lanes] + ring_sum(v2[k])[rows, lanes]
+        w[k, rows, lanes] = (v2[k, rows, lanes] + beside) * S
+    for x in range(3, X - 3):
+        sweep_one(v2, place[x], place[x - 1], place[x + 1])
+
+    for x in range(3, X - 3):
+        fo[x] = sweep_two(v2, place[x], place[x - 1], place[x + 1])
 
     passed = []
 
@@ -286,21 +311,28 @@
         passed.append(send(block, block, dev(z=Q)))
         passed[-1].start()
 
+    pass_on(gather[0], O)
     pass_on(gather[1], D)
     pass_on(gather[2], U)
 
     wait(outside2)
-    three = (2, X - 5)
+    for s in range(2):
+        k = two[s]
+        center = v2[k]
+        swept = (center + (v2[one[s]] + v2[three[s]] + ring_sum(center))) * S
+        w[k, :, Z : Z + 128] = swept[:, Z : Z + 128]
+        w[k, Y : Y + 8, lanes] = swept[Y : Y + 8, lanes]
     for s in range(2):
         sweep_one(v2, one[s], zero[s], two[s])
         center = v2[zero[s]]
         p0[s] = center + (v2[one[s]] + ring_sum(center))
     for s in range(2):
-        fo[place_of(two[s], X)] = sweep_two(v2, two[s], one[s], three[s])
+        fo[(2, X - 3)[s]] = sweep_two(v2, two[s], one[s], three[s])
         k1[s] = partial_two(v2, one[s], two[s]) + p0[s, rows, lanes] * S
         k0[s] = (v2[zero[s], rows, lanes] + w[one[s], rows, lanes]
                  + (ring_sum(p0[s])[rows, lanes] + v2[zero[s], rows, lanes]) * S)
-    pass_on(gather[0], O)
+    for copy in early:
+        copy.wait_send()
     wait(far2)
     for s in range(2):
         k0[s] = k0[s] + v2[far[s], rows, lanes] * S
@@ -315,20 +347,16 @@
 
     direct.wait_recv()
     wait(passed)
-    for copy in sends:
+    for copy in sends[len(early):]:
         copy.wait_send()
-
-
-def place_of(k, X):
-    return k + 1
 
 
 def write_out(fine, coarse, fine_hbm, coarse_hbm, sems):
     copies = []
     for src, dst in ((fine, fine_hbm), (coarse, coarse_hbm)):
-        half = src.shape[0] // 2
-        for k in range(2):
-            part = slice(k * half, (k + 1) * half)
+        for k in range(4):
+            size = src.shape[0] // 4
+            part = slice(k * size, (k + 1) * size)
             copies.append(pltpu.make_async_copy(src.at[part], dst.at[part], sems.at[len(copies)]))
     for copy in copies:
         copy.start()
@@ -382,7 +410,7 @@
                    jax.ShapeDtypeStruct(coarse_start.shape, f32)),
         in_specs=[in_vmem, in_vmem],
         out_specs=(any_space, any_space),
-        scratch_shapes=[pltpu.SemaphoreType.DMA((4,))],
+        scratch_shapes=[pltpu.SemaphoreType.DMA((8,))],
     )(fine, coarse)
 
 

time: 63 us -> 61.9 us (0.983)
  Pallas kernels: 62.2 us -> 61.1 us
    pallas_call x1, Pallas kernels: 61.2 us -> 60.1 us  [body(): pl.pallas_call(functools.partial(kernel, sizes), out_shape=(pltpu.VMEM((X...]
where the time goes in v4:
time: 61.9 us; the launch traced here: 61.7 us
  Pallas kernels  61.1 us (99%)
  between operations  0.64 us (1%)
    pallas_call x1, Pallas kernels, body(): pl.pallas_call(functools.partial(kernel, sizes), out_shape=(pltpu.VMEM((X...  60.1 us

profile of v4, /device:TPU:33, one launch (start us, length us, event | category | flops | bytes accessed | tf_op | source)
XLA Modules:
  0.0 61.7 jit_solution(14460100390540542265)
XLA Ops:
  0.6 60.1 %shard_map.50 = (f32[8,64,256]{2,1,0:T(8,128)S(1)}, f32[4,128,256]{2,1,0:T(8,128)S(1)}) custom-call(f32[8,64,256]{2,1,0:T(8,128)} %u_hbm.1, f32[2,8,64,256]{3,2,1,0:T(8,128)} %e_hbm.1, f32[4,128,256]{2,1,0:T(8,128)} %cs_hbm.1), custom_call_target="tpu_custom_call" | custom-call | tf_op jit(solution)/shard_map/pallas_call | solution.py:376
  60.7 1.0 %shard_map.51 = (f32[8,64,256]{2,1,0:T(8,128)}, f32[4,128,256]{2,1,0:T(8,128)}) custom-call(f32[8,64,256]{2,1,0:T(8,128)S(1)} %get-tuple-element.4.fine, f32[4,128,256]{2,1,0:T(8,128)S(1)} %get-tuple-element.5.coarse), custom_call_target="tpu_custom_call" | custom-call | tf_op jit(solution)/shard_map/pallas_call | solution.py:407

commit v5 on v4

--- a/solution.py
+++ b/solution.py
@@ -285,8 +285,10 @@
         for s in range(2):
             total = (k0[s, part] + v1[far[s], part, lanes] * S) * S
             v2[zero[s], part, lanes] = reaction(total, e[1, ends[s], part], FINE_STEP)
-        corner2 += start(send_corner_rows(v2, half))
-        near2 += start(send_near(v2, part))
+        edge, plane = send_corner_rows(v2, half), send_near(v2, part)
+        start(*((edge, plane) if half else (plane, edge)))
+        corner2 += edge
+        near2 += plane
     pack(v2, 1)
     corner2 += start(send_packed(1))
     planes(X - 4, X, lambda k: z_select(v2, zs2, k))

time: 61.9 us -> 61.9 us (level)
  no operation moved by 1% of the time
where the time goes in v5:
time: 61.9 us; the launch traced here: 61.7 us
  Pallas kernels  61.1 us (99%)
  between operations  0.64 us (1%)
    pallas_call x1, Pallas kernels, body(): pl.pallas_call(functools.partial(kernel, sizes), out_shape=(pltpu.VMEM((X...  60.1 us

profile of v5, /device:TPU:33, one launch (start us, length us, event | category | flops | bytes accessed | tf_op | source)
XLA Modules:
  0.0 61.7 jit_solution(16803241199281512111)
XLA Ops:
  0.6 60.1 %shard_map.50 = (f32[8,64,256]{2,1,0:T(8,128)S(1)}, f32[4,128,256]{2,1,0:T(8,128)S(1)}) custom-call(f32[8,64,256]{2,1,0:T(8,128)} %u_hbm.1, f32[2,8,64,256]{3,2,1,0:T(8,128)} %e_hbm.1, f32[4,128,256]{2,1,0:T(8,128)} %cs_hbm.1), custom_call_target="tpu_custom_call" | custom-call | tf_op jit(solution)/shard_map/pallas_call | solution.py:378
  60.7 1.0 %shard_map.51 = (f32[8,64,256]{2,1,0:T(8,128)}, f32[4,128,256]{2,1,0:T(8,128)}) custom-call(f32[8,64,256]{2,1,0:T(8,128)S(1)} %get-tuple-element.4.fine, f32[4,128,256]{2,1,0:T(8,128)S(1)} %get-tuple-element.5.coarse), custom_call_target="tpu_custom_call" | custom-call | tf_op jit(solution)/shard_map/pallas_call | solution.py:409
